TPU v7x, 512 devices: a whole 4x4x16 slice. The times are simulated.
512 devices in a mesh: crop: 8 (over z_lo, core), axial: 64 (over x, y, z_hi).
Axes of the slice: x: 4, y: 4, z: 16 (z_hi: 4, z_lo: 4; z = z_hi * 4 + z_lo), core: 2. Of those that a mesh axis runs over, the one named last changes fastest.
Arguments:
- pair: bfloat16 [8, 256, 256, 128], P('crop', 'axial'), may hold values from -6 to 6
- crop_mask: int32 [8, 256], P('crop'), may hold values 0 or 1
- weights: bfloat16 [128, 768], replicated, may hold values from -0.5 to 0.5
- probe_signs: int32 [128, 768], replicated, may hold values from 0 to 1
Outputs:
- pair_out: bfloat16 [8, 256, 256, 128], P('crop', 'axial')
- curvature: float32 [128, 768], replicated
All inputs are finite; a program needn't handle non-finite values. No bound on the sum of `crop_mask` on one device may be relied on, other than what follows from the above.
Results may differ from a plain program's by a relative error of at most 0.006.
Values may be sent and summed in bfloat16 or wider, within the bound.
A program may use at most 64 MiB of HBM per device.

v0:
```python
import jax
import jax.numpy as jnp
from jax import lax
from jax.sharding import PartitionSpec as P


def norm_axis(value, axis):
    mean = jnp.mean(value, axis=axis, keepdims=True)
    centered = value - mean
    var = jnp.mean(centered * centered, axis=axis, keepdims=True)
    return centered * lax.rsqrt(var + 1e-05)


def project_in(w_in, zn_bf, mask_pair):
    proj = jnp.einsum(
        "rnc,cd->drn", zn_bf, w_in.astype(jnp.bfloat16), preferred_element_type=jnp.float32
    )
    hid = proj.shape[0] // 4
    a_full = jax.nn.sigmoid(proj[hid : 2 * hid]) * proj[:hid] * mask_pair
    b_full = jax.nn.sigmoid(proj[3 * hid :]) * proj[2 * hid : 3 * hid] * mask_pair
    return (a_full, b_full)


def head(w_head, x_full, zn_bf):
    chans = zn_bf.shape[2]
    w_gate = w_head[:, :chans].astype(jnp.bfloat16)
    w_out = w_head[:, chans:].astype(jnp.bfloat16)
    x_norm = norm_axis(x_full, 0).astype(jnp.bfloat16)
    out_proj = jnp.einsum("hrn,hc->rnc", x_norm, w_out, preferred_element_type=jnp.float32)
    gating = jax.nn.sigmoid(
        jnp.einsum("rnc,cd->rnd", zn_bf, w_gate, preferred_element_type=jnp.float32)
    )
    return gating * out_proj


def tri_out(left, right):
    return jnp.einsum("cik,cjk->cij", left, right, preferred_element_type=jnp.float32)


def slab_products(slabs):
    a_ch, b_ch, ta_ch, tb_ch = slabs
    x_ch = tri_out(a_ch, b_ch).astype(jnp.bfloat16)
    tx_ch = (tri_out(ta_ch, b_ch) + tri_out(a_ch, tb_ch)).astype(jnp.bfloat16)
    return (x_ch, tx_ch, a_ch, b_ch)


def shards(pair, crop_mask, weights, probe_signs):
    pair_rows = pair[0]
    rows = pair_rows.shape[0]
    width = pair_rows.shape[1]
    chans = weights.shape[0]
    h4 = weights.shape[1] - 2 * chans
    mask = crop_mask[0].astype(jnp.float32)
    start = lax.axis_index("axial") * rows
    mask_rows = lax.dynamic_slice_in_dim(mask, start, rows, 0)
    mask_pair = mask_rows[:, None] * mask[None, :]
    zn = norm_axis(pair_rows.astype(jnp.float32), 2).astype(jnp.bfloat16)
    w_all = weights.astype(jnp.float32)
    probe = (2 * probe_signs - 1).astype(jnp.float32) * (1.0 / jnp.sqrt(jnp.float32(chans)))
    w_in, w_head = (w_all[:, :h4], w_all[:, h4:])
    v_in, v_head = (probe[:, :h4], probe[:, h4:])
    fin = lambda w: project_in(w, zn, mask_pair)
    (a_f, b_f), pull_in = jax.vjp(fin, w_in)
    _, (ta_f, tb_f) = jax.jvp(fin, (w_in,), (v_in,))
    a_bf, b_bf = (a_f.astype(jnp.bfloat16), b_f.astype(jnp.bfloat16))
    ta_bf, tb_bf = (ta_f.astype(jnp.bfloat16), tb_f.astype(jnp.bfloat16))
    a_ch, b_ch = (
        lax.all_to_all(a_bf, "axial", split_axis=0, concat_axis=1, tiled=True),
        lax.all_to_all(b_bf, "axial", split_axis=0, concat_axis=1, tiled=True),
    )
    ta_ch, tb_ch = (
        lax.all_to_all(ta_bf, "axial", split_axis=0, concat_axis=1, tiled=True),
        lax.all_to_all(tb_bf, "axial", split_axis=0, concat_axis=1, tiled=True),
    )
    x_ch, tx_ch, a_ch, b_ch = slab_products((a_ch, b_ch, ta_ch, tb_ch))
    x_bf, tx_bf = (
        lax.all_to_all(x_ch, "axial", split_axis=1, concat_axis=0, tiled=True),
        lax.all_to_all(tx_ch, "axial", split_axis=1, concat_axis=0, tiled=True),
    )
    fhead = lambda w, xx: head(w, xx, zn)
    out, pull_head = jax.vjp(fhead, w_head, x_bf.astype(jnp.float32))
    _, t_out = jax.jvp(
        fhead, (w_head, x_bf.astype(jnp.float32)), (v_head, tx_bf.astype(jnp.float32))
    )
    total = lax.axis_size("crop") * width * width
    cot = t_out * (1.0 / total)
    g_head, x_bar = pull_head(cot)
    g_head_sum = lax.psum(g_head, ("crop", "axial"))
    xb_ch = lax.all_to_all(
        x_bar.astype(jnp.bfloat16), "axial", split_axis=0, concat_axis=1, tiled=True
    )
    a_bar = jnp.einsum("cij,cjk->cik", xb_ch, b_ch, preferred_element_type=jnp.float32).astype(
        jnp.bfloat16
    )
    b_bar = jnp.einsum("cij,cik->cjk", xb_ch, a_ch, preferred_element_type=jnp.float32).astype(
        jnp.bfloat16
    )
    a_back, b_back = (
        lax.all_to_all(a_bar, "axial", split_axis=1, concat_axis=0, tiled=True),
        lax.all_to_all(b_bar, "axial", split_axis=1, concat_axis=0, tiled=True),
    )
    g_in = pull_in((a_back.astype(jnp.float32), b_back.astype(jnp.float32)))[0]
    g_in_sum = lax.psum(g_in, ("crop", "axial"))
    curvature = jnp.concatenate([g_in_sum, g_head_sum], axis=1)
    new_pair = (pair_rows.astype(jnp.float32) + out).astype(jnp.bfloat16)
    return (new_pair[None], curvature)


def solution(mesh):
    placed = (P("crop", "axial", None, None), P("crop", None), P(), P())
    return jax.shard_map(
        shards,
        mesh=mesh,
        in_specs=placed,
        out_specs=(P("crop", "axial", None, None), P()),
        check_vma=False,
    )
```

profile of v0, /device:TPU:1, one launch (start us, length us, event | category | flops | bytes accessed | tf_op | source)
XLA Modules:
  0.0 778.7 jit_solution(10818521390159609590)
XLA Ops:
  13.0 1.8 fusion.63
  15.0 2.1 fusion.38
  18.0 21.7 %all-to-all-start.4 = ((bf16[128,4,256]{2,1,0:T(4,128)(2,1)}), bf16[128,4,256]{2,1,0:T(4,128)(2,1)S(1)}, u32[]{:S(2)}, u32[]{:S(2)}) async-start(bf16[128,4,256]{2,1,0:T(4,128)(2,1)} %copy.69), calls=%async_computation.4 | async-start | bytes 524288 | tf_op jit(solution)/shard_map/all_to_all | solution.py:73
  40.6 17.3 %all-to-all-done.4 = bf16[128,4,256]{2,1,0:T(4,128)(2,1)S(1)} async-done(((bf16[128,4,256]{2,1,0:T(4,128)(2,1)}), bf16[128,4,256]{2,1,0:T(4,128)(2,1)S(1)}, u32[]{:S(2)}, u32[]{:S(2)}) %all-to-all-start.4) | async-done | bytes 262176 | tf_op jit(solution)/shard_map/all_to_all | solution.py:73
  57.9 8.4 %all-to-all-start.1 = ((bf16[128,4,256]{2,1,0:T(4,128)(2,1)}), bf16[128,4,256]{2,1,0:T(4,128)(2,1)S(1)}, u32[]{:S(2)}, u32[]{:S(2)}) async-start(bf16[128,4,256]{2,1,0:T(4,128)(2,1)} %copy.57), calls=%async_computation.1 | async-start | bytes 524288 | tf_op jit(solution)/shard_map/all_to_all | solution.py:69
  67.1 16.5 %all-to-all-done.1 = bf16[128,4,256]{2,1,0:T(4,128)(2,1)S(1)} async-done(((bf16[128,4,256]{2,1,0:T(4,128)(2,1)}), bf16[128,4,256]{2,1,0:T(4,128)(2,1)S(1)}, u32[]{:S(2)}, u32[]{:S(2)}) %all-to-all-start.1) | async-done | bytes 262176 | tf_op jit(solution)/shard_map/all_to_all | solution.py:69
  83.6 4.6 all-to-all-start
  89.1 16.5 %all-to-all-done = bf16[128,4,256]{2,1,0:T(4,128)(2,1)S(1)} async-done(((bf16[128,4,256]{2,1,0:T(4,128)(2,1)}), bf16[128,4,256]{2,1,0:T(4,128)(2,1)S(1)}, u32[]{:S(2)}, u32[]{:S(2)}) %all-to-all-start) | async-done | bytes 262176 | tf_op jit(solution)/shard_map/all_to_all | solution.py:68
  105.6 5.5 all-to-all-start.3
  113.8 14.6 %all-to-all-done.3 = bf16[128,4,256]{2,1,0:T(4,128)(2,1)} async-done(((bf16[128,4,256]{2,1,0:T(4,128)(2,1)}), bf16[128,4,256]{2,1,0:T(4,128)(2,1)}, u32[]{:S(2)}, u32[]{:S(2)}) %all-to-all-start.3) | async-done | bytes 262176 | tf_op jit(solution)/shard_map/all_to_all | solution.py:72
  128.3 4.6 all-to-all-start.2
  134.8 1.7 copy.66
  136.5 1.7 all_to_all.105
  140.7 9.6 %all-to-all-done.2 = bf16[2,256,256]{2,0,1:T(2,128)(2,1)S(1)} async-done(((bf16[2,256,256]{2,0,1:T(2,128)(2,1)}), bf16[2,256,256]{2,0,1:T(2,128)(2,1)S(1)}, u32[]{:S(2)}, u32[]{:S(2)}) %all-to-all-start.2) | async-done | bytes 262176 | tf_op jit(solution)/shard_map/all_to_all | solution.py:77
  150.3 7.8 %all-to-all-start.5 = ((bf16[2,256,256]{2,0,1:T(2,128)(2,1)}), bf16[2,256,256]{2,0,1:T(2,128)(2,1)}, u32[]{:S(2)}, u32[]{:S(2)}) async-start(bf16[2,256,256]{2,0,1:T(2,128)(2,1)} %copy.71), calls=%async_computation.5 | async-start | bytes 524288 | tf_op jit(solution)/shard_map/all_to_all | solution.py:78
  163.8 13.4 %all-to-all-done.5 = bf16[2,256,256]{2,0,1:T(2,128)(2,1)} async-done(((bf16[2,256,256]{2,0,1:T(2,128)(2,1)}), bf16[2,256,256]{2,0,1:T(2,128)(2,1)}, u32[]{:S(2)}, u32[]{:S(2)}) %all-to-all-start.5) | async-done | bytes 262176 | tf_op jit(solution)/shard_map/all_to_all | solution.py:78
  179.3 1.9 copy_bitcast_fusion
  181.3 2.2 reshape.106
  183.5 1.9 multiply_reduce_fusion
  191.5 22.6 %all_to_all.126 = bf16[128,4,256]{2,1,0:T(4,128)(2,1)S(1)} all-to-all(bf16[128,4,256]{2,1,0:T(4,128)(2,1)S(1)} %copy.75), channel_id=1, replica_groups=mesh['crop'=8,'axial'=64] {'axial'}, dimensions={0} | all-to-all | bytes 524288 | tf_op jit(solution)/shard_map/all_to_all | solution.py:89
  215.9 5.5 all-to-all-start.8
  223.7 20.0 %all-to-all-done.8 = bf16[2,256,256]{2,0,1:T(2,128)(2,1)} async-done(((bf16[2,256,256]{2,0,1:T(2,128)(2,1)}), bf16[2,256,256]{2,0,1:T(2,128)(2,1)}, u32[]{:S(2)}, u32[]{:S(2)}) %all-to-all-start.8) | async-done | bytes 262176 | tf_op jit(solution)/shard_map/all_to_all | solution.py:99
  243.7 5.5 all-to-all-start.7
  250.6 1.6 fusion.28
  252.9 1.8 copy.83
  254.7 2.0 copy.84
  256.8 9.8 %all-to-all-done.7 = bf16[2,256,256]{2,0,1:T(2,128)(2,1)} async-done(((bf16[2,256,256]{2,0,1:T(2,128)(2,1)}), bf16[2,256,256]{2,0,1:T(2,128)(2,1)}, u32[]{:S(2)}, u32[]{:S(2)}) %all-to-all-start.7) | async-done | bytes 262176 | tf_op jit(solution)/shard_map/all_to_all | solution.py:100
  266.6 1.8 copy.79
  268.4 2.1 copy.80
  270.5 1.6 multiply_multiply_fusion.3
  274.3 495.7 %all-reduce.9.cloned.1.call-done = (f32[128,256]{1,0:T(8,128)}, f32[128,512]{1,0:T(8,128)}) async-done(((f32[128,256]{1,0:T(8,128)}, f32[128,512]{1,0:T(8,128)}), (f32[128,256]{1,0:T(8,128)}, f32[128,512]{1,0:T(8,128)})) %all-reduce.9.cloned.1.call-update) | async-done | bytes 393232 | tf_op jit(solution)/shard_map/psum | solution.py:88
  770.0 1.8 pad_maximum_fusion
  (85 shorter events, 38.4 us)
Async XLA Ops:
  7.2 5.8 copy-start
  11.4 3.4 copy-start.14
  18.0 39.9 %all-to-all-start.4 = ((bf16[128,4,256]{2,1,0:T(4,128)(2,1)}), bf16[128,4,256]{2,1,0:T(4,128)(2,1)S(1)}, u32[]{:S(2)}, u32[]{:S(2)}) async-start(bf16[128,4,256]{2,1,0:T(4,128)(2,1)} %copy.69), calls=%async_computation.4 | async-start | bytes 524288 | tf_op jit(solution)/shard_map/all_to_all | solution.py:73
  57.9 25.8 %all-to-all-start.1 = ((bf16[128,4,256]{2,1,0:T(4,128)(2,1)}), bf16[128,4,256]{2,1,0:T(4,128)(2,1)S(1)}, u32[]{:S(2)}, u32[]{:S(2)}) async-start(bf16[128,4,256]{2,1,0:T(4,128)(2,1)} %copy.57), calls=%async_computation.1 | async-start | bytes 524288 | tf_op jit(solution)/shard_map/all_to_all | solution.py:69
  83.6 22.0 %all-to-all-start = ((bf16[128,4,256]{2,1,0:T(4,128)(2,1)}), bf16[128,4,256]{2,1,0:T(4,128)(2,1)S(1)}, u32[]{:S(2)}, u32[]{:S(2)}) async-start(bf16[128,4,256]{2,1,0:T(4,128)(2,1)} %copy.55), calls=%async_computation | async-start | bytes 524288 | tf_op jit(solution)/shard_map/all_to_all | solution.py:68
  105.6 5.5 copy-start.13
  105.6 22.7 %all-to-all-start.3 = ((bf16[128,4,256]{2,1,0:T(4,128)(2,1)}), bf16[128,4,256]{2,1,0:T(4,128)(2,1)}, u32[]{:S(2)}, u32[]{:S(2)}) async-start(bf16[128,4,256]{2,1,0:T(4,128)(2,1)} %copy.65), calls=%async_computation.3 | async-start | bytes 524288 | tf_op jit(solution)/shard_map/all_to_all | solution.py:72
  111.3 26.9 %copy-start.8 = (bf16[2,256,256]{2,1,0:T(8,128)(2,1)}, bf16[2,256,256]{2,1,0:T(8,128)(2,1)S(1)}, u32[]{:S(2)}) copy-start(bf16[2,256,256]{2,1,0:T(8,128)(2,1)S(1)} %all_to_all.100) | copy-start | bytes 786436
  112.5 26.9 %copy-start.6 = (bf16[2,256,256]{2,1,0:T(8,128)(2,1)}, bf16[2,256,256]{2,1,0:T(8,128)(2,1)S(1)}, u32[]{:S(2)}) copy-start(bf16[2,256,256]{2,1,0:T(8,128)(2,1)S(1)} %all_to_all.96) | copy-start | bytes 786436
  128.3 22.0 %all-to-all-start.2 = ((bf16[2,256,256]{2,0,1:T(2,128)(2,1)}), bf16[2,256,256]{2,0,1:T(2,128)(2,1)S(1)}, u32[]{:S(2)}, u32[]{:S(2)}) async-start(bf16[2,256,256]{2,0,1:T(2,128)(2,1)} %copy.59), calls=%async_computation.2 | async-start | bytes 524288 | tf_op jit(solution)/shard_map/all_to_all | solution.py:77
  150.3 9.1 %copy-start.10 = (bf16[2,256,256]{2,0,1:T(2,128)(2,1)}, bf16[2,256,256]{2,0,1:T(2,128)(2,1)S(1)}, u32[]{:S(2)}) copy-start(bf16[2,256,256]{2,0,1:T(2,128)(2,1)S(1)} %all-to-all-done.2) | copy-start | bytes 786436
  150.3 26.9 %all-to-all-start.5 = ((bf16[2,256,256]{2,0,1:T(2,128)(2,1)}), bf16[2,256,256]{2,0,1:T(2,128)(2,1)}, u32[]{:S(2)}, u32[]{:S(2)}) async-start(bf16[2,256,256]{2,0,1:T(2,128)(2,1)} %copy.71), calls=%async_computation.5 | async-start | bytes 524288 | tf_op jit(solution)/shard_map/all_to_all | solution.py:78
  162.9 0.8 copy-start.4
  178.4 0.8 copy-start.5
  183.5 3.0 copy-start.12
  185.5 2.2 copy-start.7
  186.5 3.4 copy-start.1
  189.9 1.4 copy-start.3
  191.0 23.3 %copy-start.9 = (bf16[2,256,256]{2,1,0:T(8,128)(2,1)S(1)}, bf16[2,256,256]{2,1,0:T(8,128)(2,1)}, u32[]{:S(2)}) copy-start(bf16[2,256,256]{2,1,0:T(8,128)(2,1)} %copy-done.8) | copy-start | bytes 786436
  214.3 0.7 copy-start.11
  215.0 35.7 %copy-start.2 = (f32[4,256,128]{2,1,0:T(8,128)S(1)}, f32[4,256,128]{2,1,0:T(8,128)}, u32[]{:S(2)}) copy-start(f32[4,256,128]{2,1,0:T(8,128)} %copy-done.1) | copy-start | bytes 1572868
  215.9 27.8 %all-to-all-start.8 = ((bf16[2,256,256]{2,0,1:T(2,128)(2,1)}), bf16[2,256,256]{2,0,1:T(2,128)(2,1)}, u32[]{:S(2)}, u32[]{:S(2)}) async-start(bf16[2,256,256]{2,0,1:T(2,128)(2,1)} %copy.82), calls=%async_computation.8 | async-start | bytes 524288 | tf_op jit(solution)/shard_map/all_to_all | solution.py:99
  243.7 22.8 %all-to-all-start.7 = ((bf16[2,256,256]{2,0,1:T(2,128)(2,1)}), bf16[2,256,256]{2,0,1:T(2,128)(2,1)}, u32[]{:S(2)}, u32[]{:S(2)}) async-start(bf16[2,256,256]{2,0,1:T(2,128)(2,1)} %copy.78), calls=%async_computation.7 | async-start | bytes 524288 | tf_op jit(solution)/shard_map/all_to_all | solution.py:100
  249.2 520.8 %all-reduce.9.cloned.1.call-start = ((), (), s32[]{:S(2)}) async-start(), calls=%async_computation.9 | async-start | bytes 786432 | tf_op jit(solution)/shard_map/psum | solution.py:88
Sparse Core Ops, SparseCore 0:
  273.7 496.2 all-reduce.8
where the time goes:
time: 781 us; the launch traced here: 779 us
  waiting for transfers between devices  613 us (78%)
  starting transfers between devices  63.6 us (8%)
  local copies, waits for them, and re-layouts  28.1 us (4%)
  blocking collectives  22.6 us (3%)
  other arithmetic  18.9 us (2%)
  matrix products  17.7 us (2%)
  between operations  14.5 us (2%)
    psum x1, waiting for transfers between devices, shards(): g_head_sum = lax.psum(g_head, ('crop', 'axial'))  496 us
    all_to_all x1, blocking collectives, shards(): lax.all_to_all(x_bar.astype(jnp.bfloat16), 'axial', split_axis=0, concat_...  22.6 us
    all_to_all x1, starting transfers between devices, shards(): lax.all_to_all(tb_bf, 'axial', split_axis=0, concat_axis=1, tiled=True)  21.7 us
    all_to_all x1, waiting for transfers between devices, shards(): lax.all_to_all(a_bar, 'axial', split_axis=1, concat_axis=0, tiled=True)  20 us
    all_to_all x1, waiting for transfers between devices, shards(): lax.all_to_all(tb_bf, 'axial', split_axis=0, concat_axis=1, tiled=True)  17.3 us
    all_to_all x1, waiting for transfers between devices, shards(): lax.all_to_all(b_bf, 'axial', split_axis=0, concat_axis=1, tiled=True)  16.5 us
    all_to_all x1, waiting for transfers between devices, shards(): lax.all_to_all(a_bf, 'axial', split_axis=0, concat_axis=1, tiled=True)  16.5 us
  transfers between devices with their start and end apart: 9, of which 9 were waited for; matrix products, arithmetic and copies ran while one was open for 3% of the time, Pallas kernels for 0%

commit v1 on v0

v1 whole, which is shorter than its diff:
```python
import jax
import jax.numpy as jnp
from jax import lax
from jax.experimental import pallas as pl
from jax.experimental.pallas import tpu as pltpu
from jax.sharding import PartitionSpec as P

MESH = pl.DeviceIdType.MESH
F32 = jnp.float32
BF16 = jnp.bfloat16
EPS = 1e-05
TOTAL = 8 * 256 * 256
NT = (((1,), (1,)), ((), ()))
NN = (((1,), (0,)), ((), ()))
TN = (((0,), (0,)), ((), ()))


def dot(a, b, dims):
    return lax.dot_general(a, b, dims, preferred_element_type=F32)


def mean0(value):
    return jnp.mean(value, axis=0, keepdims=True)


def loop(lo, hi, body):
    def step(i, carry):
        body(i)
        return carry

    lax.fori_loop(lo, hi, step, 0)


def kernel(
    pair_ref, cmask_ref, w_ref, s_ref,
    out_ref, curv_ref,
    wt, vt, wq, pg, mk, zn, fac, tmp,
    sf, rf, xs, xr, zs, zr, outs, xb4, xbr, xbs, rx, as_, ar,
    gg, hs, hr, gi, us, ur, vb, wb, ft,
    mv_s, mv_r, ag_s, ag_r, xs_s, xs_r, q_s, q_r, v_s, v_r, o_s, o_r, l_s,
):
    crop = lax.axis_index("crop")
    axial = lax.axis_index("axial")
    xy = lax.div(axial, 4)
    hi = lax.rem(axial, 4)
    half = lax.div(crop, 4)
    q = lax.rem(crop, 4)
    v = 2 * hi + half

    def dev(c, a):
        return {"crop": c, "axial": a}

    def xy_dev(p):
        return dev(crop, 4 * p + hi)

    def q_dev(p):
        return dev(4 * half + p, axial)

    def v_dev(p):
        return dev(4 * lax.rem(p, 2) + q, 4 * xy + lax.div(p, 2))

    dst_c = 4 * lax.rem(crop, 2) + hi
    dst_a = 4 * xy + lax.div(crop, 2)
    src_c = 2 * hi + half
    src_a = 4 * xy + q
    moved = jnp.logical_or(dst_c != crop, dst_a != axial)
    stays = jnp.logical_not(moved)

    def rcopy(src, dst, ssem, rsem, to):
        return pltpu.make_async_remote_copy(
            src_ref=src, dst_ref=dst, send_sem=ssem, recv_sem=rsem,
            device_id=to, device_id_type=MESH,
        )

    barrier = pltpu.get_barrier_semaphore()

    def greet(to):
        pl.semaphore_signal(barrier, inc=1, device_id=to, device_id_type=MESH)

    loop(1, 16, lambda d: greet(xy_dev(lax.rem(xy + d, 16))))
    loop(1, 8, lambda d: greet(v_dev(lax.rem(v + d, 8))))
    loop(1, 4, lambda d: greet(q_dev(lax.rem(q + d, 4))))

    @pl.when(moved)
    def _():
        greet(dev(dst_c, dst_a))
        greet(dev(src_c, src_a))

    for t in range(6):
        cols = slice(128 * t, 128 * t + 128)
        wt[cols, :] = w_ref[:, cols].astype(F32).T.astype(BF16)
        probe = (2 * s_ref[:, cols] - 1).astype(F32) * (1.0 / jnp.sqrt(F32(128)))
        vt[cols, :] = probe.T.astype(BF16)
    for t in range(4):
        rows = pl.ds(pl.multiple_of(128 * t + 32 * q, 32), 32)
        wq[32 * t : 32 * t + 32, :] = wt[rows, :]
        wq[128 + 32 * t : 160 + 32 * t, :] = vt[rows, :]

    @pl.when(moved)
    def _():
        pl.semaphore_wait(barrier, 27)

    @pl.when(stays)
    def _():
        pl.semaphore_wait(barrier, 25)

    def put(lo, val):
        for k in range(2):
            tmp[pl.ds(2048 * k + lo, 32, stride=16), :] = val[:, 128 * k : 128 * k + 128]

    def get(lo):
        parts = [tmp[pl.ds(2048 * k + lo, 32, stride=16), :] for k in range(2)]
        return jnp.concatenate(parts, axis=1)

    def put_flat(i, val):
        for k in range(2):
            rows = pl.ds(pl.multiple_of(2048 * k + 128 * i, 128), 128)
            tmp[rows, :] = val[:, 128 * k : 128 * k + 128]

    def get_flat(i):
        parts = [
            tmp[pl.ds(pl.multiple_of(2048 * k + 128 * i, 128), 128), :] for k in range(2)
        ]
        return jnp.concatenate(parts, axis=1).reshape(8, 16, 256)

    def mv_pair():
        return rcopy(
            pair_ref, pg.at[pl.ds(4 * hi, 4)], mv_s.at[0], mv_r.at[0], dev(dst_c, dst_a)
        )

    def mv_mask():
        return rcopy(cmask_ref, mk, mv_s.at[1], mv_r.at[1], dev(dst_c, dst_a))

    @pl.when(moved)
    def _():
        mv_pair().start()
        mv_mask().start()
        mv_pair().wait()
        mv_mask().wait()

    @pl.when(stays)
    def _():
        one = pltpu.make_async_copy(pair_ref, pg.at[pl.ds(4 * q, 4)], l_s.at[0])
        two = pltpu.make_async_copy(cmask_ref, mk, l_s.at[1])
        one.start()
        two.start()
        one.wait()
        two.wait()

    q1 = q + 1 - 2 * lax.rem(q, 2)
    q2 = lax.rem(q + 2, 4)
    q3 = lax.rem(q1 + 2, 4)

    def block(p):
        return pg.at[pl.ds(4 * p, 4)]

    near = rcopy(block(q), block(q), ag_s.at[0], ag_r.at[0], q_dev(q1))
    far = rcopy(block(q), block(q), ag_s.at[1], ag_r.at[1], q_dev(q2))
    pass_on = rcopy(block(q2), block(q2), ag_s.at[2], ag_r.at[2], q_dev(q1))
    far.start()
    near.start()

    lanes = lax.broadcasted_iota(jnp.int32, (1, 256), 1)

    def project(r):
        rows = pg[r].astype(F32)
        centered = rows - jnp.mean(rows, axis=1, keepdims=True)
        var = jnp.mean(centered * centered, axis=1, keepdims=True)
        znr = (centered * lax.rsqrt(var + EPS)).astype(BF16)
        zn[r] = znr
        proj = dot(wq[...], znr, NT)
        m = mk[...].astype(F32)
        mi = jnp.sum(jnp.where(lanes == 16 * xy + r, m, 0.0), axis=1, keepdims=True)
        mrow = m * mi
        for side in range(2):
            lo = 64 * side
            p, g = proj[lo : lo + 32], proj[lo + 32 : lo + 64]
            tp, tg = proj[128 + lo : 160 + lo], proj[160 + lo : 192 + lo]
            s = jax.nn.sigmoid(g)
            fp = s * mrow
            fg = p * (fp * (1.0 - s))
            fac[r, lo : lo + 32, :] = fp
            fac[r, lo + 32 : lo + 64, :] = fg
            put(512 * side + r, fp * p)
            put(1024 + 512 * side + r, fg * tg + fp * tp)

    loop(0, 4, lambda i: project(4 * q + i))
    far.wait_recv()
    pass_on.start()
    loop(0, 4, lambda i: project(4 * q2 + i))
    near.wait_recv()
    loop(0, 4, lambda i: project(4 * q1 + i))
    pass_on.wait_recv()
    loop(0, 4, lambda i: project(4 * q3 + i))
    near.wait_send()
    far.wait_send()
    pass_on.wait_send()

    def xy_start(n, src, dst):
        pltpu.make_async_copy(src(xy), dst(xy), l_s.at[0]).start()

        def send(d):
            p = lax.rem(xy + d, 16)
            rcopy(src(p), dst(xy), xs_s.at[n, p], xs_r.at[n, xy], xy_dev(p)).start()

        loop(1, 16, send)

    def xy_wait(n, src, dst):
        pltpu.make_async_copy(src(xy), dst(xy), l_s.at[0]).wait()

        def done(d):
            p = lax.rem(xy + d, 16)
            both = rcopy(src(p), dst(p), xs_s.at[n, p], xs_r.at[n, p], xy_dev(p))
            both.wait_send()
            both.wait_recv()

        loop(1, 16, done)

    def q_start(n, src, dst):
        pltpu.make_async_copy(src(q), dst(q), l_s.at[1 + n]).start()

        def send(d):
            p = lax.rem(q + d, 4)
            rcopy(src(p), dst(q), q_s.at[n, p], q_r.at[n, q], q_dev(p)).start()

        loop(1, 4, send)

    def q_wait(n, src, dst):
        pltpu.make_async_copy(src(q), dst(q), l_s.at[1 + n]).wait()

        def done(d):
            p = lax.rem(q + d, 4)
            both = rcopy(src(p), dst(p), q_s.at[n, p], q_r.at[n, p], q_dev(p))
            both.wait_send()
            both.wait_recv()

        loop(1, 4, done)

    def rows_of(p, n):
        return pl.ds(pl.multiple_of(n * p, n), n)

    def pack(i):
        sf[lax.div(i, 4), pl.ds(8 * lax.rem(i, 4), 8)] = get_flat(i).astype(BF16)

    loop(0, 16, pack)
    one = (0, lambda p: sf.at[:, pl.ds(2 * p, 2)], lambda p: rf.at[:, :, rows_of(p, 16), :])
    xy_start(*one)
    xy_wait(*one)

    for c in range(2):
        x = dot(rf[0, c], rf[1, c], NT)
        tx = dot(rf[2, c], rf[1, c], NT) + dot(rf[0, c], rf[3, c], NT)
        xs[0, c] = x.astype(BF16)
        xs[1, c] = tx.astype(BF16)

    two = (1, lambda p: xs.at[:, :, rows_of(p, 16), :], lambda p: xr.at[:, pl.ds(2 * p, 2)])
    xy_start(*two)
    xy_wait(*two)

    def spread(src):
        def body(i):
            val = src[lax.div(i, 4), pl.ds(8 * lax.rem(i, 4), 8)].astype(F32)
            put_flat(i, val.reshape(128, 256))

        loop(0, 8, body)

    spread(xr)

    def turn(r):
        zs[0, r] = get(r).astype(BF16)
        zs[1, r] = get(512 + r).astype(BF16)

    loop(0, 16, turn)
    three = (0, lambda p: zs.at[:, pl.ds(4 * p, 4)], lambda p: zr.at[:, :, rows_of(p, 32), :])
    q_start(*three)
    q_wait(*three)

    gg[...] = jnp.zeros_like(gg)
    hs[...] = jnp.zeros_like(hs)

    def head(r):
        znr = zn[4 * q + r]
        x = zr[0, r].astype(F32)
        tx = zr[1, r].astype(F32)
        c = x - mean0(x)
        rs = lax.rsqrt(mean0(c * c) + EPS)
        xnb = (c * rs).astype(BF16)
        tc = tx - mean0(tx)
        slope = -0.5 * (rs * rs * rs)
        drs = slope * mean0(2.0 * c * tc)
        dxnb = (tc * rs + c * drs).astype(BF16)
        g = dot(wt[512:640, :], znr, NT)
        dg = dot(vt[512:640, :], znr, NT)
        w_out = wt[640:768, :]
        out = dot(w_out, xnb, NN)
        dout = dot(w_out, dxnb, NN) + dot(vt[640:768, :], xnb, NN)
        s = jax.nn.sigmoid(g)
        sp = s * (1.0 - s)
        y = s * out
        ybar = (sp * dg * out + s * dout) * (1.0 / TOTAL)
        gbar = (ybar * out * sp).astype(BF16)
        obar = (ybar * s).astype(BF16)
        hs[0:128, :] += dot(gbar, znr, NN)
        hs[128:256, :] += dot(obar, xnb, NT)
        xnbar = dot(w_ref[:, 640:768], obar, NN).astype(BF16).astype(F32)
        rsbar = jnp.sum(xnbar * c, axis=0, keepdims=True)
        cbar = xnbar * rs + c * (rsbar * slope * (2.0 / 128))
        xb4[r] = (cbar - mean0(cbar)).astype(BF16)
        outs[r] = (pg[4 * q + r].astype(F32) + y.T).astype(BF16)

    loop(0, 4, head)

    four = (1, lambda p: xb4.at[:, rows_of(p, 32), :], lambda p: xbr.at[pl.ds(4 * p, 4)])
    five = (2, lambda p: hs.at[rows_of(p, 64), :], lambda p: hr.at[p])
    q_start(*four)

    def back():
        return rcopy(outs, out_ref, o_s, o_r, dev(src_c, src_a))

    def keep():
        return pltpu.make_async_copy(outs, out_ref, o_s)

    @pl.when(moved)
    def _():
        back().start()

    @pl.when(stays)
    def _():
        keep().start()

    q_wait(*four)
    q_start(*five)

    def turn_back(r):
        put(r, xbr[r].astype(F32))

    loop(0, 16, turn_back)

    def pack_back(i):
        xbs[pl.ds(8 * i, 8)] = get_flat(i).astype(BF16)

    loop(0, 4, pack_back)
    six = (2, lambda p: xbs.at[pl.ds(2 * p, 2)], lambda p: rx.at[:, rows_of(p, 16), :])
    xy_start(*six)
    xy_wait(*six)

    for c in range(2):
        as_[0, c] = dot(rx[c], rf[1, c], NN).astype(BF16)
        as_[1, c] = dot(rx[c], rf[0, c], TN).astype(BF16)

    seven = (3, lambda p: as_.at[:, :, rows_of(p, 16), :], lambda p: ar.at[:, pl.ds(2 * p, 2)])
    xy_start(*seven)
    q_wait(*five)
    xy_wait(*seven)
    spread(ar)
    gi[...] = jnp.zeros_like(gi)

    def grad(r):
        ab = get(r)
        bb = get(512 + r)
        d = (fac[r] * jnp.concatenate([ab, ab, bb, bb], axis=0)).astype(BF16)
        gi[...] += dot(d, zn[r], NN)

    loop(0, 16, grad)

    gg[...] = hr[0] + hr[1] + hr[2] + hr[3]
    for p in range(16):
        us[p, 0] = gi[8 * p : 8 * p + 4, :]
        us[p, 1] = gi[8 * p + 4 : 8 * p + 8, :]
        us[p, 2] = gg[4 * p : 4 * p + 4, :]
    eight = (4, lambda p: us.at[p], lambda p: ur.at[p])
    xy_start(*eight)
    xy_wait(*eight)
    total = ur[0]
    for p in range(1, 16):
        total = total + ur[p]
    vb[v] = total

    def v_copy(d, slot):
        p = lax.rem(v + d, 8)
        mine = v if slot else p
        return rcopy(vb.at[v], vb.at[mine], v_s.at[p], v_r.at[mine], v_dev(p))

    loop(1, 8, lambda d: v_copy(d, True).start())

    def v_done(d):
        both = v_copy(d, False)
        both.wait_send()
        both.wait_recv()

    loop(1, 8, v_done)
    total = vb[0]
    for p in range(1, 8):
        total = total + vb[p]
    wb[q, xy] = total

    def gather(d, mine):
        p = lax.rem(xy + d, 16)
        slot = xy if mine else p
        return rcopy(wb.at[q, xy], wb.at[q, slot], xs_s.at[5, p], xs_r.at[5, slot], xy_dev(p))

    loop(1, 16, lambda d: gather(d, True).start())

    def gathered(d):
        both = gather(d, False)
        both.wait_send()
        both.wait_recv()

    loop(1, 16, gathered)

    def column(d, mine):
        p = lax.rem(q + d, 4)
        slot = q if mine else p
        return rcopy(wb.at[q], wb.at[slot], q_s.at[3, p], q_r.at[3, slot], q_dev(p))

    loop(1, 4, lambda d: column(d, True).start())

    def columned(d):
        both = column(d, False)
        both.wait_send()
        both.wait_recv()

    loop(1, 4, columned)
    for p in range(4):
        for k in range(16):
            lo = 128 * (k // 4) + 32 * p + 8 * (k % 4)
            ft[lo : lo + 4, :] = wb[p, k, 0]
            ft[lo + 4 : lo + 8, :] = wb[p, k, 1]
            lo = 512 + 64 * p + 4 * k
            ft[lo : lo + 4, :] = wb[p, k, 2]
    for t in range(6):
        cols = slice(128 * t, 128 * t + 128)
        curv_ref[:, cols] = ft[cols, :].T

    @pl.when(moved)
    def _():
        back().wait()

    @pl.when(stays)
    def _():
        keep().wait()


def shards(pair, crop_mask, weights, probe_signs):
    vmem = pl.BlockSpec(memory_space=pltpu.VMEM)
    dma = pltpu.SemaphoreType.DMA
    out, curv = pl.pallas_call(
        kernel,
        out_shape=(
            jax.ShapeDtypeStruct((4, 256, 128), BF16),
            jax.ShapeDtypeStruct((128, 768), F32),
        ),
        in_specs=[vmem] * 4,
        out_specs=(pl.BlockSpec(memory_space=pl.ANY), vmem),
        scratch_shapes=[
            pltpu.VMEM((768, 128), BF16),
            pltpu.VMEM((768, 128), BF16),
            pltpu.VMEM((256, 128), BF16),
            pltpu.VMEM((16, 256, 128), BF16),
            pltpu.VMEM((1, 256), jnp.int32),
            pltpu.VMEM((16, 256, 128), BF16),
            pltpu.VMEM((16, 128, 256), F32),
            pltpu.VMEM((4096, 128), F32),
            pltpu.VMEM((4, 32, 16, 256), BF16),
            pltpu.VMEM((4, 2, 256, 256), BF16),
            pltpu.VMEM((2, 2, 256, 256), BF16),
            pltpu.VMEM((2, 32, 16, 256), BF16),
            pltpu.VMEM((2, 16, 32, 256), BF16),
            pltpu.VMEM((2, 4, 128, 256), BF16),
            pltpu.VMEM((4, 256, 128), BF16),
            pltpu.VMEM((4, 128, 256), BF16),
            pltpu.VMEM((16, 32, 256), BF16),
            pltpu.VMEM((32, 16, 256), BF16),
            pltpu.VMEM((2, 256, 256), BF16),
            pltpu.VMEM((2, 2, 256, 256), BF16),
            pltpu.VMEM((2, 32, 16, 256), BF16),
            pltpu.VMEM((64, 128), F32),
            pltpu.VMEM((256, 128), F32),
            pltpu.VMEM((4, 64, 128), F32),
            pltpu.VMEM((128, 128), F32),
            pltpu.VMEM((16, 3, 4, 128), F32),
            pltpu.VMEM((16, 3, 4, 128), F32),
            pltpu.VMEM((8, 3, 4, 128), F32),
            pltpu.VMEM((4, 16, 3, 4, 128), F32),
            pltpu.VMEM((768, 128), F32),
            dma((2,)), dma((2,)), dma((3,)), dma((3,)),
            dma((6, 16)), dma((6, 16)), dma((4, 4)), dma((4, 4)),
            dma((8,)), dma((8,)), dma, dma, dma((4,)),
        ],
        compiler_params=pltpu.CompilerParams(
            collective_id=0, has_side_effects=True, vmem_limit_bytes=48 * 2**20
        ),
    )(pair[0], crop_mask, weights, probe_signs)
    return out[None], curv


def solution(mesh):
    placed = (P("crop", "axial", None, None), P("crop", None), P(), P())
    return jax.shard_map(
        shards,
        mesh=mesh,
        in_specs=placed,
        out_specs=(P("crop", "axial", None, None), P()),
        check_vma=False,
    )
```

time: 781 us -> 147 us (0.19)
  waiting for transfers between devices: 613 us -> 0 us
  Pallas kernels: 0 us -> 141 us
  starting transfers between devices: 63.6 us -> 0 us
  local copies, waits for them, and re-layouts: 28.1 us -> 4.99 us
  blocking collectives: 22.6 us -> 0 us
  other arithmetic: 18.9 us -> 0 us
  matrix products: 17.7 us -> 0 us
  between operations: 14.5 us -> 0.65 us
    psum x1 -> x0, waiting for transfers between devices: 496 us -> none  [shards(): g_head_sum = lax.psum(g_head, ('crop', 'axial'))]
    pallas_call x0 -> x1, Pallas kernels: none -> 141 us  [shards(): pl.pallas_call(kernel, out_shape=(jax.ShapeDtypeStruct((4, 256, 128), BF1...]
    all_to_all x8 -> x0, waiting for transfers between devices: 118 us -> none  [the longest x1 20 us: shards(): lax.all_to_all(a_bar, 'axial', split_axis=1, concat_axis=0, tiled=True)]
    all_to_all x8 -> x0, starting transfers between devices: 63.6 us -> none  [the longest x1 21.7 us: shards(): lax.all_to_all(tb_bf, 'axial', split_axis=0, concat_axis=1, tiled=True)]
    all_to_all x1 -> x0, blocking collectives: 22.6 us -> none  [shards(): lax.all_to_all(x_bar.astype(jnp.bfloat16), 'axial', split_axis=0, concat_...]
    convert_element_type x15 -> x0, local copies, waits for them, and re-layouts: 19.1 us -> none  [the longest x4 7.8 us: shards(): g_in = pull_in((a_back.astype(jnp.float32), b_back.astype(jnp.float32)))[0]]
    dot_general x16 -> x0, matrix products: 17.7 us -> none  [the longest x5 5.55 us: head(): jnp.einsum('hrn,hc->rnc', x_norm, w_out, preferred_element_type=jnp.float32)]
    convert_element_type x8 -> x0, other arithmetic: 8.22 us -> none  [the longest x2 3.07 us: shards(): tx_bf.astype(jnp.float32)]
  transfers between devices with their start and end apart: 9 -> 0, of which waited for: 9 -> 0; matrix products, arithmetic and copies ran while one was open for 3% -> 0% of each run, Pallas kernels for 0% -> 0%
where the time goes in v1:
time: 147 us; the launch traced here: 146 us
  Pallas kernels  141 us (96%)
  local copies, waits for them, and re-layouts  4.99 us (3%)
    pallas_call x1, Pallas kernels, shards(): pl.pallas_call(kernel, out_shape=(jax.ShapeDtypeStruct((4, 256, 128), BF1...  141 us
    unnamed x10, local copies, waits for them, and re-layouts  4.99 us

profile of v1, /device:TPU:1, one launch (start us, length us, event | category | flops | bytes accessed | tf_op | source)
XLA Modules:
  0.0 146.4 jit_solution(6528374671356468331)
XLA Ops:
  0.6 0.0 copy-start.3
  0.6 0.7 copy-done.3
  1.3 0.0 copy-start
  1.3 1.0 copy-done
  2.3 0.0 copy-start.1
  2.3 0.9 copy-done.1
  3.3 0.0 copy-start.2
  3.3 0.9 copy-done.2
  4.2 140.8 %shard_map.59 = (bf16[4,256,128]{2,1,0:T(8,128)(2,1)S(1)}, f32[128,768]{1,0:T(8,128)S(1)}) custom-call(bf16[4,256,128]{2,1,0:T(8,128)(2,1)S(1)} %bitcast.3, s32[1,256]{1,0:T(1,128)S(1)} %copy-done.3, bf16[128,768]{1,0:T(8,128)(2,1)S(1)} %copy-done.2, s32[128,768]{1,0:T(8,128)S(1)} %copy-done), custom_call_target="tpu_custom_call" | custom-call | tf_op jit(solution)/shard_map/pallas_call | solution.py:447
  145.0 0.7 copy.8
  145.7 0.7 copy.9
Async XLA Ops:
  0.6 0.7 copy-start.3
  1.3 1.0 copy-start
  2.3 0.9 copy-start.1
  3.3 0.9 copy-start.2

commit v2 on v1

v2 whole, which is shorter than its diff:
```python
import jax
import jax.numpy as jnp
from jax import lax
from jax.experimental import pallas as pl
from jax.experimental.pallas import tpu as pltpu
from jax.sharding import PartitionSpec as P

MESH = pl.DeviceIdType.MESH
F32 = jnp.float32
BF16 = jnp.bfloat16
EPS = 1e-05
TOTAL = 8 * 256 * 256
NT = (((1,), (1,)), ((), ()))
NN = (((1,), (0,)), ((), ()))
TN = (((0,), (0,)), ((), ()))


def dot(a, b, dims):
    return lax.dot_general(a, b, dims, preferred_element_type=F32)


def mean0(value):
    return jnp.mean(value, axis=0, keepdims=True)


BLOCK_OF = (6, 2, 1, 5, 0, 4, 3, 7)
PLACE_OF = (
    (2, 3, 0, 1), (0, 1, 3, 2), (1, 3, 2, 0), (2, 1, 0, 3),
    (3, 2, 0, 1), (0, 1, 3, 2), (1, 2, 3, 0), (3, 0, 1, 2),
)


def table(index, values):
    found = 0
    for k, value in enumerate(values):
        found = found + jnp.where(index == k, value, 0)
    return found


def loop(lo, hi, body):
    def step(i, carry):
        body(i)
        return carry

    lax.fori_loop(lo, hi, step, 0)


def kernel(
    pair_ref, cmask_ref, w_any, s_any,
    out_ref, curv_ref,
    pv, cm, w_ref, s_ref,
    wt, vt, wq, pg, mk, zn, fac, tmp,
    sf, rf, xs, xr, zs, zr, outs, xb4, xbr, xbs, rx, as_, ar,
    hsum, hs, hr, gi, us, ur, vb, wb, ft,
    in_s, mv_s, mv_r, ag_s, ag_r, xs_s, xs_r, q_s, q_r, v_s, v_r, o_s, o_r, lx_s, lq_s,
):
    crop = lax.axis_index("crop")
    axial = lax.axis_index("axial")
    xy = lax.div(axial, 4)
    hi = lax.rem(axial, 4)
    half = lax.div(crop, 4)
    q = lax.rem(crop, 4)
    v = 2 * hi + half

    def dev(c, a):
        return {"crop": c, "axial": a}

    def xy_dev(p):
        return dev(crop, 4 * p + hi)

    def q_dev(p):
        return dev(4 * half + p, axial)

    def v_dev(p):
        return dev(4 * lax.rem(p, 2) + q, 4 * xy + lax.div(p, 2))

    dst = table(
        4 * crop + hi, [4 * BLOCK_OF[c] + PLACE_OF[c][k] for c in range(8) for k in range(4)]
    )
    home = {4 * BLOCK_OF[c] + PLACE_OF[c][k]: 4 * c + k for c in range(8) for k in range(4)}
    homes = [home[k] for k in range(32)]
    src = table(4 * v + q, homes)
    slots = [table(v, [homes[4 * b + p] % 4 for b in range(8)]) for p in range(4)]

    def slot(p):
        return table(p, slots)

    dst_v, dst_q = lax.div(dst, 4), lax.rem(dst, 4)
    dst_c = 4 * lax.rem(dst_v, 2) + dst_q
    dst_a = 4 * xy + lax.div(dst_v, 2)
    src_c = lax.div(src, 4)
    src_a = 4 * xy + lax.rem(src, 4)
    moved = dst != 4 * v + q
    stays = jnp.logical_not(moved)

    def rcopy(src, dst, ssem, rsem, to):
        return pltpu.make_async_remote_copy(
            src_ref=src, dst_ref=dst, send_sem=ssem, recv_sem=rsem,
            device_id=to, device_id_type=MESH,
        )

    barrier = pltpu.get_barrier_semaphore()

    def greet(to):
        pl.semaphore_signal(barrier, inc=1, device_id=to, device_id_type=MESH)

    loop(1, 16, lambda d: greet(xy_dev(lax.rem(xy + d, 16))))
    loop(1, 8, lambda d: greet(v_dev(lax.rem(v + d, 8))))
    loop(1, 4, lambda d: greet(q_dev(lax.rem(q + d, 4))))

    @pl.when(moved)
    def _():
        greet(dev(dst_c, dst_a))
        greet(dev(src_c, src_a))

    loads = [
        pltpu.make_async_copy(a, b, in_s.at[k])
        for k, (a, b) in enumerate(
            ((w_any, w_ref), (s_any, s_ref), (cmask_ref, cm), (pair_ref, pv))
        )
    ]
    for load in loads:
        load.start()
    loads[0].wait()
    loads[1].wait()
    for t in range(6):
        cols = slice(128 * t, 128 * t + 128)
        wt[cols, :] = w_ref[:, cols].astype(F32).T.astype(BF16)
        probe = (2 * s_ref[:, cols] - 1).astype(F32) * (1.0 / jnp.sqrt(F32(128)))
        vt[cols, :] = probe.T.astype(BF16)
    for t in range(4):
        rows = pl.ds(pl.multiple_of(128 * t + 32 * q, 32), 32)
        wq[32 * t : 32 * t + 32, :] = wt[rows, :]
        wq[128 + 32 * t : 160 + 32 * t, :] = vt[rows, :]
    loads[2].wait()
    loads[3].wait()

    @pl.when(moved)
    def _():
        pl.semaphore_wait(barrier, 27)

    @pl.when(stays)
    def _():
        pl.semaphore_wait(barrier, 25)

    def put(k, lo, val):
        tmp[pl.ds(2048 * k + lo, 32, stride=16), :] = val

    def get(k, lo):
        return tmp[pl.ds(2048 * k + lo, 32, stride=16), :]

    def flat(k, i):
        return pl.ds(pl.multiple_of(2048 * k + 128 * i, 128), 128)

    def spread(k, src):
        def body(i):
            val = src[k, lax.div(i, 4), pl.ds(8 * lax.rem(i, 4), 8)].astype(F32)
            tmp[flat(k, i), :] = val.reshape(128, 128)

        loop(0, 8, body)

    own = slot(q)

    def lanes_of(k):
        return slice(128 * k, 128 * k + 128)

    def mv_pair(k):
        return rcopy(
            pv.at[:, lanes_of(k)], pg.at[pl.ds(4 * hi, 4), lanes_of(k)],
            mv_s.at[k], mv_r.at[k], dev(dst_c, dst_a),
        )

    def mv_mask():
        return rcopy(cm, mk, mv_s.at[2], mv_r.at[2], dev(dst_c, dst_a))

    def own_pair(k):
        return pltpu.make_async_copy(
            pv.at[:, lanes_of(k)], pg.at[pl.ds(4 * own, 4), lanes_of(k)], mv_r.at[k]
        )

    def own_mask():
        return pltpu.make_async_copy(cm, mk, mv_r.at[2])

    @pl.when(moved)
    def _():
        mv_mask().start()
        mv_pair(0).start()
        mv_pair(1).start()

    @pl.when(stays)
    def _():
        own_mask().start()
        own_pair(0).start()
        own_pair(1).start()

    q1 = q + 1 - 2 * lax.rem(q, 2)
    q2 = lax.rem(q + 2, 4)
    q3 = lax.rem(q1 + 2, 4)

    def block(k, p):
        return pg.at[pl.ds(4 * slot(p), 4), lanes_of(k)]

    def near(k):
        return rcopy(block(k, q), block(k, q), ag_s.at[k, 0], ag_r.at[k, 0], q_dev(q1))

    def far(k):
        return rcopy(block(k, q), block(k, q), ag_s.at[k, 1], ag_r.at[k, 1], q_dev(q2))

    def pass_on(k):
        return rcopy(block(k, q2), block(k, q2), ag_s.at[k, 2], ag_r.at[k, 2], q_dev(q1))

    def arrived(k):
        @pl.when(moved)
        def _():
            if k == 0:
                mv_mask().wait()
            mv_pair(k).wait()

        @pl.when(stays)
        def _():
            if k == 0:
                own_mask().wait()
            own_pair(k).wait()

    iota = lax.broadcasted_iota(jnp.int32, (1, 256), 1)

    def project(k, r):
        rows = pg[r, lanes_of(k), :].astype(F32)
        centered = rows - jnp.mean(rows, axis=1, keepdims=True)
        var = jnp.mean(centered * centered, axis=1, keepdims=True)
        znr = (centered * lax.rsqrt(var + EPS)).astype(BF16)
        zn[r, lanes_of(k), :] = znr
        proj = dot(wq[...], znr, NT)
        m = mk[...].astype(F32)
        mi = jnp.sum(jnp.where(iota == 16 * xy + r, m, 0.0), axis=1, keepdims=True)
        mrow = m[:, lanes_of(k)] * mi
        for side in range(2):
            lo = 64 * side
            p, g = proj[lo : lo + 32], proj[lo + 32 : lo + 64]
            tp, tg = proj[128 + lo : 160 + lo], proj[160 + lo : 192 + lo]
            s = jax.nn.sigmoid(g)
            fp = s * mrow
            fg = p * (fp * (1.0 - s))
            fac[k, r, lo : lo + 32, :] = fp
            fac[k, r, lo + 32 : lo + 64, :] = fg
            put(k, 512 * side + r, fp * p)
            put(k, 1024 + 512 * side + r, fg * tg + fp * tp)

    def project4(k, p):
        for i in range(4):
            project(k, 4 * p + i)

    def xy_start(n, src, dst):
        pltpu.make_async_copy(src(xy), dst(xy), lx_s.at[n]).start()

        def send(d):
            p = lax.rem(xy + d, 16)
            rcopy(src(p), dst(xy), xs_s.at[n, p], xs_r.at[n, xy], xy_dev(p)).start()

        loop(1, 16, send)

    def xy_wait(n, src, dst):
        pltpu.make_async_copy(src(xy), dst(xy), lx_s.at[n]).wait()

        def done(d):
            p = lax.rem(xy + d, 16)
            both = rcopy(src(p), dst(p), xs_s.at[n, p], xs_r.at[n, p], xy_dev(p))
            both.wait_send()
            both.wait_recv()

        loop(1, 16, done)

    def q_start(n, src, dst):
        pltpu.make_async_copy(src(q), dst(q), lq_s.at[n]).start()

        def send(d):
            p = lax.rem(q + d, 4)
            rcopy(src(p), dst(q), q_s.at[n, p], q_r.at[n, q], q_dev(p)).start()

        loop(1, 4, send)

    def q_wait(n, src, dst):
        pltpu.make_async_copy(src(q), dst(q), lq_s.at[n]).wait()

        def done(d):
            p = lax.rem(q + d, 4)
            both = rcopy(src(p), dst(p), q_s.at[n, p], q_r.at[n, p], q_dev(p))
            both.wait_send()
            both.wait_recv()

        loop(1, 4, done)

    def rows_of(p, n):
        return pl.ds(pl.multiple_of(n * p, n), n)

    def ab(k):
        return (
            k,
            lambda p: sf.at[k, :, pl.ds(2 * p, 2)],
            lambda p: rf.at[k, :, :, rows_of(p, 16), :],
        )

    for k in range(2):
        arrived(k)
        far(k).start()
        near(k).start()
        project4(k, slot(q))
        near(k).wait_recv()
        project4(k, slot(q1))
        far(k).wait_recv()
        pass_on(k).start()
        project4(k, slot(q2))
        pass_on(k).wait_recv()
        project4(k, slot(q3))

        def pack(i):
            val = tmp[flat(k, i), :].reshape(8, 16, 128)
            sf[k, lax.div(i, 4), pl.ds(8 * lax.rem(i, 4), 8)] = val.astype(BF16)

        loop(0, 16, pack)
        xy_start(*ab(k))
    for k in range(2):
        near(k).wait_send()
        far(k).wait_send()
        pass_on(k).wait_send()
    for k in range(2):
        xy_wait(*ab(k))

    def xx(k):
        return (
            2 + k,
            lambda p: xs.at[k, :, :, rows_of(p, 16), :],
            lambda p: xr.at[k, :, pl.ds(2 * p, 2)],
        )

    def both(ref, *at):
        return jnp.concatenate([ref[(0, *at)], ref[(1, *at)]], axis=1)

    for k in range(2):
        for c in range(2):
            a, b, ta, tb = [both(rf, n, c) for n in range(4)]
            b, tb = b[lanes_of(k)], tb[lanes_of(k)]
            x = dot(a, b, NT)
            tx = dot(jnp.concatenate([ta, a], axis=1), jnp.concatenate([b, tb], axis=1), NT)
            xs[k, 0, c] = x.astype(BF16)
            xs[k, 1, c] = tx.astype(BF16)
        xy_start(*xx(k))

    def zz(k):
        return (
            k,
            lambda p: zs.at[k, :, pl.ds(4 * slot(p), 4)],
            lambda p: zr.at[k, :, :, rows_of(p, 32), :],
        )

    for k in range(2):
        xy_wait(*xx(k))
        spread(k, xr)

        def turn(r):
            zs[k, 0, r] = get(k, r).astype(BF16)
            zs[k, 1, r] = get(k, 512 + r).astype(BF16)

        loop(0, 16, turn)
        q_start(*zz(k))

    hs[...] = jnp.zeros_like(hs)

    def head(k, r):
        znr = zn[4 * own + r, lanes_of(k), :]
        x = zr[k, 0, r].astype(F32)
        tx = zr[k, 1, r].astype(F32)
        c = x - mean0(x)
        rs = lax.rsqrt(mean0(c * c) + EPS)
        xnb = (c * rs).astype(BF16)
        tc = tx - mean0(tx)
        slope = -0.5 * (rs * rs * rs)
        drs = slope * mean0(2.0 * c * tc)
        dxnb = (tc * rs + c * drs).astype(BF16)
        g = dot(wt[512:640, :], znr, NT)
        dg = dot(vt[512:640, :], znr, NT)
        w_out = wt[640:768, :]
        out = dot(w_out, xnb, NN)
        dout = dot(w_out, dxnb, NN) + dot(vt[640:768, :], xnb, NN)
        s = jax.nn.sigmoid(g)
        sp = s * (1.0 - s)
        y = s * out
        ybar = (sp * dg * out + s * dout) * (1.0 / TOTAL)
        gbar = (ybar * out * sp).astype(BF16)
        obar = (ybar * s).astype(BF16)
        xnbar = dot(w_ref[:, 640:768], obar, NN).astype(BF16).astype(F32)
        rsbar = jnp.sum(xnbar * c, axis=0, keepdims=True)
        cbar = xnbar * rs + c * (rsbar * slope * (2.0 / 128))
        xb4[k, r] = (cbar - mean0(cbar)).astype(BF16)
        row = pg[4 * own + r, lanes_of(k), :].astype(F32)
        outs[r, lanes_of(k), :] = (row + y.T).astype(BF16)
        return dot(gbar, znr, NN), dot(obar, xnb, NT)

    def heads(k, i):
        first, second = head(k, 2 * i), head(k, 2 * i + 1)
        hs[0:128, :] += first[0] + second[0]
        hs[128:256, :] += first[1] + second[1]

    def xb(k):
        return (
            2 + k,
            lambda p: xb4.at[k, :, rows_of(p, 32), :],
            lambda p: xbr.at[k, pl.ds(4 * slot(p), 4)],
        )

    five = (4, lambda p: hs.at[rows_of(p, 64), :], lambda p: hr.at[p])
    for k in range(2):
        q_wait(*zz(k))
        loop(0, 2, lambda i: heads(k, i))
        q_start(*xb(k))

    def back():
        return rcopy(outs, out_ref, o_s, o_r, dev(src_c, src_a))

    def keep():
        return pltpu.make_async_copy(outs, out_ref, o_s)

    def rr(k):
        return (
            4 + k,
            lambda p: xbs.at[k, pl.ds(2 * p, 2)],
            lambda p: rx.at[k, :, rows_of(p, 16), :],
        )

    for k in range(2):
        q_wait(*xb(k))
        loop(0, 16, lambda r: put(k, r, xbr[k, r].astype(F32)))

        def pack_back(i):
            val = tmp[flat(k, i), :].reshape(8, 16, 128)
            xbs[k, pl.ds(8 * i, 8)] = val.astype(BF16)

        loop(0, 4, pack_back)
        xy_start(*rr(k))

    q_start(*five)

    @pl.when(moved)
    def _():
        back().start()

    @pl.when(stays)
    def _():
        keep().start()

    for k in range(2):
        xy_wait(*rr(k))

    def aa(k):
        return (
            6 + k,
            lambda p: as_.at[k, :, :, rows_of(p, 16), :],
            lambda p: ar.at[k, :, pl.ds(2 * p, 2)],
        )

    for c in range(2):
        xbar = both(rx, c)
        abar = dot(xbar, both(rf, 1, c), NN).astype(BF16)
        bbar = dot(xbar, both(rf, 0, c), TN).astype(BF16)
        for k in range(2):
            as_[k, 0, c] = abar[:, lanes_of(k)]
            as_[k, 1, c] = bbar[:, lanes_of(k)]
    for k in range(2):
        xy_start(*aa(k))

    gi[...] = jnp.zeros_like(gi)
    q_wait(*five)
    hsum[...] = hr[0] + hr[1] + hr[2] + hr[3]
    for k in range(2):
        xy_wait(*aa(k))
        spread(k, ar)

        def grad(r):
            ra = get(k, r)
            rb = get(k, 512 + r)
            d = (fac[k, r] * jnp.concatenate([ra, ra, rb, rb], axis=0)).astype(BF16)
            return dot(d, zn[r, lanes_of(k), :], NN)

        def grads(i):
            gi[...] += (grad(4 * i) + grad(4 * i + 1)) + (grad(4 * i + 2) + grad(4 * i + 3))

        loop(0, 4, grads)

    for p in range(16):
        us[p, 0] = gi[8 * p : 8 * p + 4, :]
        us[p, 1] = gi[8 * p + 4 : 8 * p + 8, :]
        us[p, 2] = hsum[4 * p : 4 * p + 4, :]
    eight = (8, lambda p: us.at[p], lambda p: ur.at[p])
    xy_start(*eight)
    xy_wait(*eight)
    total = ur[0]
    for p in range(1, 16):
        total = total + ur[p]
    vb[v] = total

    def v_copy(d, slot):
        p = lax.rem(v + d, 8)
        mine = v if slot else p
        return rcopy(vb.at[v], vb.at[mine], v_s.at[p], v_r.at[mine], v_dev(p))

    loop(1, 8, lambda d: v_copy(d, True).start())

    def v_done(d):
        both = v_copy(d, False)
        both.wait_send()
        both.wait_recv()

    loop(1, 8, v_done)
    total = vb[0]
    for p in range(1, 8):
        total = total + vb[p]
    wb[q, xy] = total

    def gather(d, mine):
        p = lax.rem(xy + d, 16)
        slot = xy if mine else p
        return rcopy(wb.at[q, xy], wb.at[q, slot], xs_s.at[9, p], xs_r.at[9, slot], xy_dev(p))

    loop(1, 16, lambda d: gather(d, True).start())

    def gathered(d):
        both = gather(d, False)
        both.wait_send()
        both.wait_recv()

    loop(1, 16, gathered)

    def col(p, n, to):
        return rcopy(wb.at[p], wb.at[p], ag_s.at[2, n], ag_r.at[2, n], q_dev(to))

    col(q, 1, q2).start()
    col(q, 0, q1).start()
    col(q, 1, q2).wait_recv()
    col(q2, 2, q1).start()
    col(q, 0, q1).wait()
    col(q2, 2, q1).wait()
    col(q, 1, q2).wait_send()
    for p in range(4):
        for k in range(16):
            lo = 128 * (k // 4) + 32 * p + 8 * (k % 4)
            ft[lo : lo + 4, :] = wb[p, k, 0]
            ft[lo + 4 : lo + 8, :] = wb[p, k, 1]
            lo = 512 + 64 * p + 4 * k
            ft[lo : lo + 4, :] = wb[p, k, 2]
    for t in range(6):
        cols = slice(128 * t, 128 * t + 128)
        curv_ref[:, cols] = ft[cols, :].T

    @pl.when(moved)
    def _():
        back().wait()

    @pl.when(stays)
    def _():
        keep().wait()


def shards(pair, crop_mask, weights, probe_signs):
    vmem = pl.BlockSpec(memory_space=pltpu.VMEM)
    dma = pltpu.SemaphoreType.DMA
    out, curv = pl.pallas_call(
        kernel,
        out_shape=(
            jax.ShapeDtypeStruct((4, 256, 128), BF16),
            jax.ShapeDtypeStruct((128, 768), F32),
        ),
        in_specs=[pl.BlockSpec(memory_space=pl.ANY)] * 4,
        out_specs=(pl.BlockSpec(memory_space=pl.ANY), vmem),
        scratch_shapes=[
            pltpu.VMEM((4, 256, 128), BF16),
            pltpu.VMEM((1, 256), jnp.int32),
            pltpu.VMEM((128, 768), BF16),
            pltpu.VMEM((128, 768), jnp.int32),
            pltpu.VMEM((768, 128), BF16),
            pltpu.VMEM((768, 128), BF16),
            pltpu.VMEM((256, 128), BF16),
            pltpu.VMEM((16, 256, 128), BF16),
            pltpu.VMEM((1, 256), jnp.int32),
            pltpu.VMEM((16, 256, 128), BF16),
            pltpu.VMEM((2, 16, 128, 128), F32),
            pltpu.VMEM((4096, 128), F32),
            pltpu.VMEM((2, 4, 32, 16, 128), BF16),
            pltpu.VMEM((2, 4, 2, 256, 128), BF16),
            pltpu.VMEM((2, 2, 2, 256, 128), BF16),
            pltpu.VMEM((2, 2, 32, 16, 128), BF16),
            pltpu.VMEM((2, 2, 16, 32, 128), BF16),
            pltpu.VMEM((2, 2, 4, 128, 128), BF16),
            pltpu.VMEM((4, 256, 128), BF16),
            pltpu.VMEM((2, 4, 128, 128), BF16),
            pltpu.VMEM((2, 16, 32, 128), BF16),
            pltpu.VMEM((2, 32, 16, 128), BF16),
            pltpu.VMEM((2, 2, 256, 128), BF16),
            pltpu.VMEM((2, 2, 2, 256, 128), BF16),
            pltpu.VMEM((2, 2, 32, 16, 128), BF16),
            pltpu.VMEM((64, 128), F32),
            pltpu.VMEM((256, 128), F32),
            pltpu.VMEM((4, 64, 128), F32),
            pltpu.VMEM((128, 128), F32),
            pltpu.VMEM((16, 3, 4, 128), F32),
            pltpu.VMEM((16, 3, 4, 128), F32),
            pltpu.VMEM((8, 3, 4, 128), F32),
            pltpu.VMEM((4, 16, 3, 4, 128), F32),
            pltpu.VMEM((768, 128), F32),
            dma((4,)), dma((3,)), dma((3,)), dma((3, 3)), dma((3, 3)),
            dma((10, 16)), dma((10, 16)), dma((5, 4)), dma((5, 4)),
            dma((8,)), dma((8,)), dma, dma, dma((9,)), dma((5,)),
        ],
        compiler_params=pltpu.CompilerParams(
            collective_id=0, has_side_effects=True, vmem_limit_bytes=48 * 2**20
        ),
    )(pair[0], crop_mask, weights, probe_signs)
    return out[None], curv


def solution(mesh):
    placed = (P("crop", "axial", None, None), P("crop", None), P(), P())
    return jax.shard_map(
        shards,
        mesh=mesh,
        in_specs=placed,
        out_specs=(P("crop", "axial", None, None), P()),
        check_vma=False,
    )
```

time: 147 us -> 126 us (0.86)
  Pallas kernels: 141 us -> 120 us
    pallas_call x1, Pallas kernels: 141 us -> 120 us  [shards(): pl.pallas_call(kernel, out_shape=(jax.ShapeDtypeStruct((4, 256, 128), BF1...]
where the time goes in v2:
time: 126 us; the launch traced here: 125 us
  Pallas kernels  120 us (95%)
  local copies, waits for them, and re-layouts  4.99 us (4%)
    pallas_call x1, Pallas kernels, shards(): pl.pallas_call(kernel, out_shape=(jax.ShapeDtypeStruct((4, 256, 128), BF1...  120 us
    unnamed x10, local copies, waits for them, and re-layouts  4.99 us

profile of v2, /device:TPU:1, one launch (start us, length us, event | category | flops | bytes accessed | tf_op | source)
XLA Modules:
  0.0 125.4 jit_solution(2038663365571776788)
XLA Ops:
  0.6 0.0 copy-start.3
  0.6 0.7 copy-done.3
  1.3 0.0 copy-start
  1.3 1.0 copy-done
  2.3 0.0 copy-start.1
  2.3 0.9 copy-done.1
  3.3 0.0 copy-start.2
  3.3 0.9 copy-done.2
  4.2 119.8 %shard_map.59 = (bf16[4,256,128]{2,1,0:T(8,128)(2,1)S(1)}, f32[128,768]{1,0:T(8,128)S(1)}) custom-call(bf16[4,256,128]{2,1,0:T(8,128)(2,1)S(1)} %bitcast.3, s32[1,256]{1,0:T(1,128)S(1)} %copy-done.3, bf16[128,768]{1,0:T(8,128)(2,1)S(1)} %copy-done.2, s32[128,768]{1,0:T(8,128)S(1)} %copy-done), custom_call_target="tpu_custom_call" | custom-call | tf_op jit(solution)/shard_map/pallas_call | solution.py:566
  124.0 0.7 copy.8
  124.7 0.7 copy.9
Async XLA Ops:
  0.6 0.7 copy-start.3
  1.3 1.0 copy-start
  2.3 0.9 copy-start.1
  3.3 0.9 copy-start.2

commit v3 on v2

--- a/solution.py
+++ b/solution.py
@@ -440,14 +440,6 @@
 
     q_start(*five)
 
-    @pl.when(moved)
-    def _():
-        back().start()
-
-    @pl.when(stays)
-    def _():
-        keep().start()
-
     for k in range(2):
         xy_wait(*rr(k))
 
@@ -467,6 +459,14 @@
             as_[k, 1, c] = bbar[:, lanes_of(k)]
     for k in range(2):
         xy_start(*aa(k))
+
+    @pl.when(moved)
+    def _():
+        back().start()
+
+    @pl.when(stays)
+    def _():
+        keep().start()
 
     gi[...] = jnp.zeros_like(gi)
     q_wait(*five)
@@ -514,12 +514,22 @@
     total = vb[0]
     for p in range(1, 8):
         total = total + vb[p]
-    wb[q, xy] = total
+    core, row = lax.rem(q, 2), lax.div(q, 2)
+    wb[core, row, xy] = total
+
+    def swap():
+        here = wb.at[core, row, xy]
+        return rcopy(here, here, ag_s.at[2, 0], ag_r.at[2, 0], q_dev(q2))
+
+    swap().start()
+    swap().wait()
 
     def gather(d, mine):
         p = lax.rem(xy + d, 16)
         slot = xy if mine else p
-        return rcopy(wb.at[q, xy], wb.at[q, slot], xs_s.at[9, p], xs_r.at[9, slot], xy_dev(p))
+        return rcopy(
+            wb.at[core, :, xy], wb.at[core, :, slot], xs_s.at[9, p], xs_r.at[9, slot], xy_dev(p)
+        )
 
     loop(1, 16, lambda d: gather(d, True).start())
 
@@ -530,23 +540,17 @@
 
     loop(1, 16, gathered)
 
-    def col(p, n, to):
-        return rcopy(wb.at[p], wb.at[p], ag_s.at[2, n], ag_r.at[2, n], q_dev(to))
-
-    col(q, 1, q2).start()
-    col(q, 0, q1).start()
-    col(q, 1, q2).wait_recv()
-    col(q2, 2, q1).start()
-    col(q, 0, q1).wait()
-    col(q2, 2, q1).wait()
-    col(q, 1, q2).wait_send()
+    share = rcopy(wb.at[core], wb.at[core], ag_s.at[2, 1], ag_r.at[2, 1], q_dev(q1))
+    share.start()
+    share.wait()
+
     for p in range(4):
         for k in range(16):
             lo = 128 * (k // 4) + 32 * p + 8 * (k % 4)
-            ft[lo : lo + 4, :] = wb[p, k, 0]
-            ft[lo + 4 : lo + 8, :] = wb[p, k, 1]
+            ft[lo : lo + 4, :] = wb[p % 2, p // 2, k, 0]
+            ft[lo + 4 : lo + 8, :] = wb[p % 2, p // 2, k, 1]
             lo = 512 + 64 * p + 4 * k
-            ft[lo : lo + 4, :] = wb[p, k, 2]
+            ft[lo : lo + 4, :] = wb[p % 2, p // 2, k, 2]
     for t in range(6):
         cols = slice(128 * t, 128 * t + 128)
         curv_ref[:, cols] = ft[cols, :].T
@@ -569,7 +573,7 @@
             jax.ShapeDtypeStruct((4, 256, 128), BF16),
             jax.ShapeDtypeStruct((128, 768), F32),
         ),
-        in_specs=[pl.BlockSpec(memory_space=pl.ANY)] * 4,
+        in_specs=[pl.BlockSpec(memory_space=pltpu.HBM)] * 4,
         out_specs=(pl.BlockSpec(memory_space=pl.ANY), vmem),
         scratch_shapes=[
             pltpu.VMEM((4, 256, 128), BF16),
@@ -604,7 +608,7 @@
             pltpu.VMEM((16, 3, 4, 128), F32),
             pltpu.VMEM((16, 3, 4, 128), F32),
             pltpu.VMEM((8, 3, 4, 128), F32),
-            pltpu.VMEM((4, 16, 3, 4, 128), F32),
+            pltpu.VMEM((2, 2, 16, 3, 4, 128), F32),
             pltpu.VMEM((768, 128), F32),
             dma((4,)), dma((3,)), dma((3,)), dma((3, 3)), dma((3, 3)),
             dma((10, 16)), dma((10, 16)), dma((5, 4)), dma((5, 4)),

time: 126 us -> 119 us (0.944)
  Pallas kernels: 120 us -> 113 us
    pallas_call x1, Pallas kernels: 120 us -> 113 us  [shards(): pl.pallas_call(kernel, out_shape=(jax.ShapeDtypeStruct((4, 256, 128), BF1...]
where the time goes in v3:
time: 119 us
  Pallas kernels  113 us (95%)
  local copies, waits for them, and re-layouts  4.99 us (4%)
    pallas_call x1, Pallas kernels, shards(): pl.pallas_call(kernel, out_shape=(jax.ShapeDtypeStruct((4, 256, 128), BF1...  113 us
    unnamed x10, local copies, waits for them, and re-layouts  4.99 us

profile of v3, /device:TPU:1, one launch (start us, length us, event | category | flops | bytes accessed | tf_op | source)
XLA Modules:
  0.0 118.6 jit_solution(16329693779999613181)
XLA Ops:
  0.6 0.0 copy-start.3
  0.6 0.7 copy-done.3
  1.3 0.0 copy-start
  1.3 1.0 copy-done
  2.3 0.0 copy-start.1
  2.3 0.9 copy-done.1
  3.3 0.0 copy-start.2
  3.3 0.9 copy-done.2
  4.2 113.0 %shard_map.59 = (bf16[4,256,128]{2,1,0:T(8,128)(2,1)S(1)}, f32[128,768]{1,0:T(8,128)S(1)}) custom-call(bf16[4,256,128]{2,1,0:T(8,128)(2,1)S(1)} %bitcast.3, s32[1,256]{1,0:T(1,128)S(1)} %copy-done.3, bf16[128,768]{1,0:T(8,128)(2,1)S(1)} %copy-done.2, s32[128,768]{1,0:T(8,128)S(1)} %copy-done), custom_call_target="tpu_custom_call" | custom-call | tf_op jit(solution)/shard_map/pallas_call | solution.py:570
  117.2 0.7 copy.8
  117.9 0.7 copy.9
Async XLA Ops:
  0.6 0.7 copy-start.3
  1.3 1.0 copy-start
  2.3 0.9 copy-start.1
  3.3 0.9 copy-start.2

commit v4 on v3

--- a/solution.py
+++ b/solution.py
@@ -23,10 +23,10 @@
     return jnp.mean(value, axis=0, keepdims=True)
 
 
-BLOCK_OF = (6, 2, 1, 5, 0, 4, 3, 7)
+BLOCK_OF = (7, 3, 5, 1, 4, 0, 6, 2)
 PLACE_OF = (
-    (2, 3, 0, 1), (0, 1, 3, 2), (1, 3, 2, 0), (2, 1, 0, 3),
-    (3, 2, 0, 1), (0, 1, 3, 2), (1, 2, 3, 0), (3, 0, 1, 2),
+    (3, 2, 0, 1), (1, 0, 3, 2), (2, 1, 0, 3), (0, 2, 3, 1),
+    (1, 0, 2, 3), (3, 2, 0, 1), (3, 1, 0, 2), (0, 3, 2, 1),
 )
 
 
@@ -185,7 +185,6 @@
     def _():
         mv_mask().start()
         mv_pair(0).start()
-        mv_pair(1).start()
 
     @pl.when(stays)
     def _():
@@ -304,6 +303,10 @@
         arrived(k)
         far(k).start()
         near(k).start()
+        if k == 0:
+            @pl.when(moved)
+            def _():
+                mv_pair(1).start()
         project4(k, slot(q))
         near(k).wait_recv()
         project4(k, slot(q1))
@@ -615,7 +618,7 @@
             dma((8,)), dma((8,)), dma, dma, dma((9,)), dma((5,)),
         ],
         compiler_params=pltpu.CompilerParams(
-            collective_id=0, has_side_effects=True, vmem_limit_bytes=48 * 2**20
+            collective_id=0, has_side_effects=True, vmem_limit_bytes=67043328
         ),
     )(pair[0], crop_mask, weights, probe_signs)
     return out[None], curv

time: 119 us -> 116 us (0.975)
  local copies, waits for them, and re-layouts: 4.99 us -> 2.47 us
    unnamed x10 -> x4, local copies, waits for them, and re-layouts: 4.99 us -> 2.47 us
where the time goes in v4:
time: 116 us; the launch traced here: 115 us
  Pallas kernels  112 us (97%)
  local copies, waits for them, and re-layouts  2.47 us (2%)
    pallas_call x1, Pallas kernels, shards(): pl.pallas_call(kernel, out_shape=(jax.ShapeDtypeStruct((4, 256, 128), BF1...  112 us
    unnamed x4, local copies, waits for them, and re-layouts  2.47 us

profile of v4, /device:TPU:1, one launch (start us, length us, event | category | flops | bytes accessed | tf_op | source)
XLA Modules:
  0.0 115.4 jit_solution(5177155779201299849)
XLA Ops:
  0.6 112.3 %shard_map.59 = (bf16[4,256,128]{2,1,0:T(8,128)(2,1)}, f32[128,768]{1,0:T(8,128)}) custom-call(bf16[4,256,128]{2,1,0:T(8,128)(2,1)} %bitcast.3, s32[1,256]{1,0:T(1,128)} %cmask_ref.1, bf16[128,768]{1,0:T(8,128)(2,1)} %w_any.1, s32[128,768]{1,0:T(8,128)} %s_any.1), custom_call_target="tpu_custom_call" | custom-call | tf_op jit(solution)/shard_map/pallas_call | solution.py:573
  112.9 0.0 copy-start
  112.9 1.7 %copy.8 = bf16[1,4,256,128]{3,2,1,0:T(8,128)(2,1)} copy(bf16[1,4,256,128]{3,2,1,0:T(8,128)(2,1)} %bitcast.2) | data formatting | bytes 524288
  114.6 0.0 copy-done
  114.6 0.7 copy.9
Async XLA Ops:
  112.9 1.7 %copy-start = (f32[128,768]{1,0:T(8,128)S(1)}, f32[128,768]{1,0:T(8,128)}, u32[]{:S(2)}) copy-start(f32[128,768]{1,0:T(8,128)} %get-tuple-element.9) | copy-start | bytes 1179652

commit v5 on v4

--- a/solution.py
+++ b/solution.py
@@ -164,62 +164,77 @@
     def lanes_of(k):
         return slice(128 * k, 128 * k + 128)
 
-    def mv_pair(k):
+    def piece(p, i):
+        return pl.ds(4 * p + 2 * (i % 2), 2), lanes_of(i // 2)
+
+    def mv_pair(i):
         return rcopy(
-            pv.at[:, lanes_of(k)], pg.at[pl.ds(4 * hi, 4), lanes_of(k)],
-            mv_s.at[k], mv_r.at[k], dev(dst_c, dst_a),
+            pv.at[piece(0, i)], pg.at[piece(hi, i)], mv_s.at[i], mv_r.at[i], dev(dst_c, dst_a)
         )
 
     def mv_mask():
-        return rcopy(cm, mk, mv_s.at[2], mv_r.at[2], dev(dst_c, dst_a))
-
-    def own_pair(k):
-        return pltpu.make_async_copy(
-            pv.at[:, lanes_of(k)], pg.at[pl.ds(4 * own, 4), lanes_of(k)], mv_r.at[k]
-        )
+        return rcopy(cm, mk, mv_s.at[4], mv_r.at[4], dev(dst_c, dst_a))
+
+    def own_pair(i):
+        return pltpu.make_async_copy(pv.at[piece(0, i)], pg.at[piece(own, i)], mv_r.at[i])
 
     def own_mask():
-        return pltpu.make_async_copy(cm, mk, mv_r.at[2])
-
-    @pl.when(moved)
-    def _():
-        mv_mask().start()
-        mv_pair(0).start()
-
-    @pl.when(stays)
-    def _():
-        own_mask().start()
-        own_pair(0).start()
-        own_pair(1).start()
+        return pltpu.make_async_copy(cm, mk, mv_r.at[4])
+
+    def launch(i):
+        @pl.when(moved)
+        def _():
+            if i == 0:
+                mv_mask().start()
+            mv_pair(i).start()
+
+        @pl.when(stays)
+        def _():
+            if i == 0:
+                own_mask().start()
+            own_pair(i).start()
+
+    launch(0)
+    launch(1)
 
     q1 = q + 1 - 2 * lax.rem(q, 2)
     q2 = lax.rem(q + 2, 4)
     q3 = lax.rem(q1 + 2, 4)
 
-    def block(k, p):
-        return pg.at[pl.ds(4 * slot(p), 4), lanes_of(k)]
-
-    def near(k):
-        return rcopy(block(k, q), block(k, q), ag_s.at[k, 0], ag_r.at[k, 0], q_dev(q1))
-
-    def far(k):
-        return rcopy(block(k, q), block(k, q), ag_s.at[k, 1], ag_r.at[k, 1], q_dev(q2))
-
-    def pass_on(k):
-        return rcopy(block(k, q2), block(k, q2), ag_s.at[k, 2], ag_r.at[k, 2], q_dev(q1))
-
-    def arrived(k):
+    def carry(p, i, n, m, to):
+        here = pg.at[piece(slot(p), i)]
+        return rcopy(here, here, ag_s.at[n, m], ag_r.at[n, m], q_dev(to))
+
+    def near(i):
+        return carry(q, i, 0, i // 2, q1)
+
+    def far(i):
+        return carry(q, i, 1, i, q2)
+
+    def pass_on(i):
+        return carry(q2, i, 2, i // 2, q1)
+
+    def all_rows(p, k, n, to):
+        here = pg.at[pl.ds(4 * slot(p), 4), lanes_of(k)]
+        return rcopy(here, here, ag_s.at[n, k], ag_r.at[n, k], q_dev(to))
+
+    def arrived(i):
         @pl.when(moved)
         def _():
-            if k == 0:
+            if i == 0:
                 mv_mask().wait()
-            mv_pair(k).wait()
+            mv_pair(i).wait()
 
         @pl.when(stays)
         def _():
-            if k == 0:
+            if i == 0:
                 own_mask().wait()
-            own_pair(k).wait()
+            own_pair(i).wait()
+
+        far(i).start()
+        near(i).start()
+        if i < 2:
+            launch(i + 2)
 
     iota = lax.broadcasted_iota(jnp.int32, (1, 256), 1)
 
@@ -249,45 +264,31 @@
         for i in range(4):
             project(k, 4 * p + i)
 
-    def xy_start(n, src, dst):
-        pltpu.make_async_copy(src(xy), dst(xy), lx_s.at[n]).start()
+    def xy_start(n, src, dst, most):
+        pltpu.make_async_copy(src(xy), dst(xy), lx_s.at[n % 2]).start()
 
         def send(d):
             p = lax.rem(xy + d, 16)
-            rcopy(src(p), dst(xy), xs_s.at[n, p], xs_r.at[n, xy], xy_dev(p)).start()
+            rcopy(src(p), dst(xy), xs_s.at[n], xs_r.at[n], xy_dev(p)).start()
 
         loop(1, 16, send)
 
-    def xy_wait(n, src, dst):
-        pltpu.make_async_copy(src(xy), dst(xy), lx_s.at[n]).wait()
-
-        def done(d):
-            p = lax.rem(xy + d, 16)
-            both = rcopy(src(p), dst(p), xs_s.at[n, p], xs_r.at[n, p], xy_dev(p))
-            both.wait_send()
-            both.wait_recv()
-
-        loop(1, 16, done)
-
-    def q_start(n, src, dst):
-        pltpu.make_async_copy(src(q), dst(q), lq_s.at[n]).start()
+    def xy_wait(n, src, dst, most):
+        pltpu.make_async_copy(src(xy), dst(xy), lx_s.at[n % 2]).wait()
+        rcopy(most, most, xs_s.at[n], xs_r.at[n], xy_dev(lax.rem(xy + 1, 16))).wait()
+
+    def q_start(n, src, dst, most):
+        pltpu.make_async_copy(src(q), dst(q), lq_s.at[n % 2]).start()
 
         def send(d):
             p = lax.rem(q + d, 4)
-            rcopy(src(p), dst(q), q_s.at[n, p], q_r.at[n, q], q_dev(p)).start()
+            rcopy(src(p), dst(q), q_s.at[n], q_r.at[n], q_dev(p)).start()
 
         loop(1, 4, send)
 
-    def q_wait(n, src, dst):
-        pltpu.make_async_copy(src(q), dst(q), lq_s.at[n]).wait()
-
-        def done(d):
-            p = lax.rem(q + d, 4)
-            both = rcopy(src(p), dst(p), q_s.at[n, p], q_r.at[n, p], q_dev(p))
-            both.wait_send()
-            both.wait_recv()
-
-        loop(1, 4, done)
+    def q_wait(n, src, dst, most):
+        pltpu.make_async_copy(src(q), dst(q), lq_s.at[n % 2]).wait()
+        rcopy(most, most, q_s.at[n], q_r.at[n], q_dev(q1)).wait()
 
     def rows_of(p, n):
         return pl.ds(pl.multiple_of(n * p, n), n)
@@ -297,35 +298,39 @@
             k,
             lambda p: sf.at[k, :, pl.ds(2 * p, 2)],
             lambda p: rf.at[k, :, :, rows_of(p, 16), :],
-        )
-
-    for k in range(2):
-        arrived(k)
-        far(k).start()
-        near(k).start()
-        if k == 0:
-            @pl.when(moved)
-            def _():
-                mv_pair(1).start()
-        project4(k, slot(q))
-        near(k).wait_recv()
-        project4(k, slot(q1))
-        far(k).wait_recv()
-        pass_on(k).start()
-        project4(k, slot(q2))
-        pass_on(k).wait_recv()
-        project4(k, slot(q3))
-
-        def pack(i):
+            rf.at[k, :, :, 0:240, :],
+        )
+
+    def pack(k):
+        def body(i):
             val = tmp[flat(k, i), :].reshape(8, 16, 128)
             sf[k, lax.div(i, 4), pl.ds(8 * lax.rem(i, 4), 8)] = val.astype(BF16)
 
-        loop(0, 16, pack)
+        loop(0, 16, body)
         xy_start(*ab(k))
-    for k in range(2):
-        near(k).wait_send()
-        far(k).wait_send()
-        pass_on(k).wait_send()
+
+    arrived(0)
+    arrived(1)
+    for k in range(2):
+        project4(k, slot(q))
+        for i in (2 * k, 2 * k + 1):
+            far(i).wait_recv()
+            pass_on(i).start()
+        project4(k, slot(q2))
+        all_rows(q, k, 0, q1).wait_recv()
+        project4(k, slot(q1))
+        if k == 0:
+            arrived(2)
+        all_rows(q2, k, 2, q1).wait_recv()
+        project4(k, slot(q3))
+        pack(k)
+        if k == 0:
+            arrived(3)
+    for k in range(2):
+        all_rows(q, k, 0, q1).wait_send()
+        all_rows(q2, k, 2, q1).wait_send()
+    for i in range(4):
+        far(i).wait_send()
     for k in range(2):
         xy_wait(*ab(k))
 
@@ -334,6 +339,7 @@
             2 + k,
             lambda p: xs.at[k, :, :, rows_of(p, 16), :],
             lambda p: xr.at[k, :, pl.ds(2 * p, 2)],
+            xr.at[k, :, 0:30],
         )
 
     def both(ref, *at):
@@ -354,6 +360,7 @@
             k,
             lambda p: zs.at[k, :, pl.ds(4 * slot(p), 4)],
             lambda p: zr.at[k, :, :, rows_of(p, 32), :],
+            zr.at[k, :, :, 0:96, :],
         )
 
     for k in range(2):
@@ -409,9 +416,10 @@
             2 + k,
             lambda p: xb4.at[k, :, rows_of(p, 32), :],
             lambda p: xbr.at[k, pl.ds(4 * slot(p), 4)],
-        )
-
-    five = (4, lambda p: hs.at[rows_of(p, 64), :], lambda p: hr.at[p])
+            xbr.at[k, 0:12],
+        )
+
+    five = (4, lambda p: hs.at[rows_of(p, 64), :], lambda p: hr.at[p], hr.at[0:3])
     for k in range(2):
         q_wait(*zz(k))
         loop(0, 2, lambda i: heads(k, i))
@@ -428,6 +436,7 @@
             4 + k,
             lambda p: xbs.at[k, pl.ds(2 * p, 2)],
             lambda p: rx.at[k, :, rows_of(p, 16), :],
+            rx.at[k, :, 0:240, :],
         )
 
     for k in range(2):
@@ -451,6 +460,7 @@
             6 + k,
             lambda p: as_.at[k, :, :, rows_of(p, 16), :],
             lambda p: ar.at[k, :, pl.ds(2 * p, 2)],
+            ar.at[k, :, 0:30],
         )
 
     for c in range(2):
@@ -493,7 +503,7 @@
         us[p, 0] = gi[8 * p : 8 * p + 4, :]
         us[p, 1] = gi[8 * p + 4 : 8 * p + 8, :]
         us[p, 2] = hsum[4 * p : 4 * p + 4, :]
-    eight = (8, lambda p: us.at[p], lambda p: ur.at[p])
+    eight = (8, lambda p: us.at[p], lambda p: ur.at[p], ur.at[0:15])
     xy_start(*eight)
     xy_wait(*eight)
     total = ur[0]
@@ -501,19 +511,12 @@
         total = total + ur[p]
     vb[v] = total
 
-    def v_copy(d, slot):
+    def v_send(d):
         p = lax.rem(v + d, 8)
-        mine = v if slot else p
-        return rcopy(vb.at[v], vb.at[mine], v_s.at[p], v_r.at[mine], v_dev(p))
-
-    loop(1, 8, lambda d: v_copy(d, True).start())
-
-    def v_done(d):
-        both = v_copy(d, False)
-        both.wait_send()
-        both.wait_recv()
-
-    loop(1, 8, v_done)
+        rcopy(vb.at[v], vb.at[v], v_s, v_r, v_dev(p)).start()
+
+    loop(1, 8, v_send)
+    rcopy(vb.at[0:7], vb.at[0:7], v_s, v_r, v_dev(lax.rem(v + 1, 8))).wait()
     total = vb[0]
     for p in range(1, 8):
         total = total + vb[p]
@@ -522,28 +525,21 @@
 
     def swap():
         here = wb.at[core, row, xy]
-        return rcopy(here, here, ag_s.at[2, 0], ag_r.at[2, 0], q_dev(q2))
+        return rcopy(here, here, ag_s.at[0, 2], ag_r.at[0, 2], q_dev(q2))
 
     swap().start()
     swap().wait()
 
-    def gather(d, mine):
+    def gather(d):
         p = lax.rem(xy + d, 16)
-        slot = xy if mine else p
-        return rcopy(
-            wb.at[core, :, xy], wb.at[core, :, slot], xs_s.at[9, p], xs_r.at[9, slot], xy_dev(p)
-        )
-
-    loop(1, 16, lambda d: gather(d, True).start())
-
-    def gathered(d):
-        both = gather(d, False)
-        both.wait_send()
-        both.wait_recv()
-
-    loop(1, 16, gathered)
-
-    share = rcopy(wb.at[core], wb.at[core], ag_s.at[2, 1], ag_r.at[2, 1], q_dev(q1))
+        here = wb.at[core, :, xy]
+        rcopy(here, here, xs_s.at[9], xs_r.at[9], xy_dev(p)).start()
+
+    loop(1, 16, gather)
+    most = wb.at[core, :, 0:15]
+    rcopy(most, most, xs_s.at[9], xs_r.at[9], xy_dev(lax.rem(xy + 1, 16))).wait()
+
+    share = rcopy(wb.at[core], wb.at[core], ag_s.at[0, 3], ag_r.at[0, 3], q_dev(q1))
     share.start()
     share.wait()
 
@@ -566,18 +562,16 @@
     def _():
         keep().wait()
 
-
 def shards(pair, crop_mask, weights, probe_signs):
-    vmem = pl.BlockSpec(memory_space=pltpu.VMEM)
     dma = pltpu.SemaphoreType.DMA
     out, curv = pl.pallas_call(
         kernel,
         out_shape=(
-            jax.ShapeDtypeStruct((4, 256, 128), BF16),
-            jax.ShapeDtypeStruct((128, 768), F32),
+            pltpu.VMEM((4, 256, 128), BF16),
+            pltpu.VMEM((128, 768), F32),
         ),
         in_specs=[pl.BlockSpec(memory_space=pltpu.HBM)] * 4,
-        out_specs=(pl.BlockSpec(memory_space=pl.ANY), vmem),
+        out_specs=(pl.BlockSpec(memory_space=pltpu.VMEM),) * 2,
         scratch_shapes=[
             pltpu.VMEM((4, 256, 128), BF16),
             pltpu.VMEM((1, 256), jnp.int32),
@@ -613,12 +607,12 @@
             pltpu.VMEM((8, 3, 4, 128), F32),
             pltpu.VMEM((2, 2, 16, 3, 4, 128), F32),
             pltpu.VMEM((768, 128), F32),
-            dma((4,)), dma((3,)), dma((3,)), dma((3, 3)), dma((3, 3)),
-            dma((10, 16)), dma((10, 16)), dma((5, 4)), dma((5, 4)),
-            dma((8,)), dma((8,)), dma, dma, dma((9,)), dma((5,)),
+            dma((4,)), dma((5,)), dma((5,)), dma((3, 4)), dma((3, 4)),
+            dma((10,)), dma((10,)), dma((5,)), dma((5,)),
+            dma, dma, dma, dma, dma((2,)), dma((2,)),
         ],
         compiler_params=pltpu.CompilerParams(
-            collective_id=0, has_side_effects=True, vmem_limit_bytes=67043328
+            collective_id=0, has_side_effects=True, vmem_limit_bytes=58 * 2**20
         ),
     )(pair[0], crop_mask, weights, probe_signs)
     return out[None], curv

time: 116 us -> 109 us (0.940)
  Pallas kernels: 112 us -> 107 us
    pallas_call x1, Pallas kernels: 112 us -> 107 us  [shards(): pl.pallas_call(kernel, out_shape=(pltpu.VMEM((4, 256, 128), BF16), pltpu....]
    unnamed x4 -> x2, local copies, waits for them, and re-layouts: 2.47 us -> 1.45 us
where the time goes in v5:
time: 109 us
  Pallas kernels  107 us (98%)
  local copies, waits for them, and re-layouts  1.45 us (1%)
    pallas_call x1, Pallas kernels, shards(): pl.pallas_call(kernel, out_shape=(pltpu.VMEM((4, 256, 128), BF16), pltpu....  107 us

profile of v5, /device:TPU:1, one launch (start us, length us, event | category | flops | bytes accessed | tf_op | source)
XLA Modules:
  0.0 108.7 jit_solution(7021561867540454899)
XLA Ops:
  0.6 106.6 %shard_map.59 = (bf16[4,256,128]{2,1,0:T(8,128)(2,1)S(1)}, f32[128,768]{1,0:T(8,128)S(1)}) custom-call(bf16[4,256,128]{2,1,0:T(8,128)(2,1)} %bitcast.3, s32[1,256]{1,0:T(1,128)} %cmask_ref.1, bf16[128,768]{1,0:T(8,128)(2,1)} %w_any.1, s32[128,768]{1,0:T(8,128)} %s_any.1), custom_call_target="tpu_custom_call" | custom-call | tf_op jit(solution)/shard_map/pallas_call | solution.py:567
  107.2 0.7 copy.8
  107.9 0.7 copy.9

commit v6 on v5

--- a/solution.py
+++ b/solution.py
@@ -27,6 +27,12 @@
 PLACE_OF = (
     (3, 2, 0, 1), (1, 0, 3, 2), (2, 1, 0, 3), (0, 2, 3, 1),
     (1, 0, 2, 3), (3, 2, 0, 1), (3, 1, 0, 2), (0, 3, 2, 1),
+)
+
+
+SHIFTS = (
+    (2, 2), (2, 1), (1, 2), (2, 3), (3, 2), (1, 1), (3, 3), (1, 3), (3, 1),
+    (2, 0), (0, 2), (1, 0), (0, 1), (3, 0), (0, 3),
 )
 
 
@@ -264,14 +270,16 @@
         for i in range(4):
             project(k, 4 * p + i)
 
+    peers = [
+        4 * lax.rem(lax.div(xy, 4) + dx, 4) + lax.rem(lax.rem(xy, 4) + dy, 4)
+        for dx, dy in SHIFTS
+    ]
+
     def xy_start(n, src, dst, most):
         pltpu.make_async_copy(src(xy), dst(xy), lx_s.at[n % 2]).start()
 
-        def send(d):
-            p = lax.rem(xy + d, 16)
+        for p in peers:
             rcopy(src(p), dst(xy), xs_s.at[n], xs_r.at[n], xy_dev(p)).start()
-
-        loop(1, 16, send)
 
     def xy_wait(n, src, dst, most):
         pltpu.make_async_copy(src(xy), dst(xy), lx_s.at[n % 2]).wait()
@@ -280,11 +288,8 @@
     def q_start(n, src, dst, most):
         pltpu.make_async_copy(src(q), dst(q), lq_s.at[n % 2]).start()
 
-        def send(d):
-            p = lax.rem(q + d, 4)
+        for p in (q2, q3, q1):
             rcopy(src(p), dst(q), q_s.at[n], q_r.at[n], q_dev(p)).start()
-
-        loop(1, 4, send)
 
     def q_wait(n, src, dst, most):
         pltpu.make_async_copy(src(q), dst(q), lq_s.at[n % 2]).wait()
@@ -511,11 +516,8 @@
         total = total + ur[p]
     vb[v] = total
 
-    def v_send(d):
-        p = lax.rem(v + d, 8)
-        rcopy(vb.at[v], vb.at[v], v_s, v_r, v_dev(p)).start()
-
-    loop(1, 8, v_send)
+    for d in (4, 3, 5, 2, 6, 1, 7):
+        rcopy(vb.at[v], vb.at[v], v_s, v_r, v_dev(lax.rem(v + d, 8))).start()
     rcopy(vb.at[0:7], vb.at[0:7], v_s, v_r, v_dev(lax.rem(v + 1, 8))).wait()
     total = vb[0]
     for p in range(1, 8):
@@ -530,12 +532,9 @@
     swap().start()
     swap().wait()
 
-    def gather(d):
-        p = lax.rem(xy + d, 16)
-        here = wb.at[core, :, xy]
+    here = wb.at[core, :, xy]
+    for p in peers:
         rcopy(here, here, xs_s.at[9], xs_r.at[9], xy_dev(p)).start()
-
-    loop(1, 16, gather)
     most = wb.at[core, :, 0:15]
     rcopy(most, most, xs_s.at[9], xs_r.at[9], xy_dev(lax.rem(xy + 1, 16))).wait()
 

time: 109 us -> 105 us (0.963)
  Pallas kernels: 107 us -> 103 us
    pallas_call x1, Pallas kernels: 107 us -> 103 us  [shards(): pl.pallas_call(kernel, out_shape=(pltpu.VMEM((4, 256, 128), BF16), pltpu....]
where the time goes in v6:
time: 105 us
  Pallas kernels  103 us (98%)
  local copies, waits for them, and re-layouts  1.45 us (1%)
    pallas_call x1, Pallas kernels, shards(): pl.pallas_call(kernel, out_shape=(pltpu.VMEM((4, 256, 128), BF16), pltpu....  103 us

profile of v6, /device:TPU:1, one launch (start us, length us, event | category | flops | bytes accessed | tf_op | source)
XLA Modules:
  0.0 104.9 jit_solution(5529069301161065946)
XLA Ops:
  0.6 102.8 %shard_map.59 = (bf16[4,256,128]{2,1,0:T(8,128)(2,1)S(1)}, f32[128,768]{1,0:T(8,128)S(1)}) custom-call(bf16[4,256,128]{2,1,0:T(8,128)(2,1)} %bitcast.3, s32[1,256]{1,0:T(1,128)} %cmask_ref.1, bf16[128,768]{1,0:T(8,128)(2,1)} %w_any.1, s32[128,768]{1,0:T(8,128)} %s_any.1), custom_call_target="tpu_custom_call" | custom-call | tf_op jit(solution)/shard_map/pallas_call | solution.py:566
  103.4 0.7 copy.8
  104.1 0.7 copy.9

commit v7 on v6

--- a/solution.py
+++ b/solution.py
@@ -158,12 +158,10 @@
     def flat(k, i):
         return pl.ds(pl.multiple_of(2048 * k + 128 * i, 128), 128)
 
-    def spread(k, src):
-        def body(i):
-            val = src[k, lax.div(i, 4), pl.ds(8 * lax.rem(i, 4), 8)].astype(F32)
-            tmp[flat(k, i), :] = val.reshape(128, 128)
-
-        loop(0, 8, body)
+    def spread(k, t, src):
+        for i in range(4):
+            val = src[k, t, 8 * i : 8 * i + 8].astype(F32)
+            tmp[flat(k, 4 * t + i), :] = val.reshape(128, 128)
 
     own = slot(q)
 
@@ -276,34 +274,35 @@
     ]
 
     def xy_start(n, src, dst, most):
-        pltpu.make_async_copy(src(xy), dst(xy), lx_s.at[n % 2]).start()
+        pltpu.make_async_copy(src(xy), dst(xy), lx_s.at[n % 4]).start()
 
         for p in peers:
             rcopy(src(p), dst(xy), xs_s.at[n], xs_r.at[n], xy_dev(p)).start()
 
     def xy_wait(n, src, dst, most):
-        pltpu.make_async_copy(src(xy), dst(xy), lx_s.at[n % 2]).wait()
+        pltpu.make_async_copy(src(xy), dst(xy), lx_s.at[n % 4]).wait()
         rcopy(most, most, xs_s.at[n], xs_r.at[n], xy_dev(lax.rem(xy + 1, 16))).wait()
 
     def q_start(n, src, dst, most):
-        pltpu.make_async_copy(src(q), dst(q), lq_s.at[n % 2]).start()
+        pltpu.make_async_copy(src(q), dst(q), lq_s.at[n]).start()
 
         for p in (q2, q3, q1):
             rcopy(src(p), dst(q), q_s.at[n], q_r.at[n], q_dev(p)).start()
 
     def q_wait(n, src, dst, most):
-        pltpu.make_async_copy(src(q), dst(q), lq_s.at[n % 2]).wait()
+        pltpu.make_async_copy(src(q), dst(q), lq_s.at[n]).wait()
         rcopy(most, most, q_s.at[n], q_r.at[n], q_dev(q1)).wait()
 
     def rows_of(p, n):
         return pl.ds(pl.multiple_of(n * p, n), n)
 
-    def ab(k):
+    def ab(t, k):
+        two = pl.ds(2 * t, 2)
         return (
-            k,
-            lambda p: sf.at[k, :, pl.ds(2 * p, 2)],
-            lambda p: rf.at[k, :, :, rows_of(p, 16), :],
-            rf.at[k, :, :, 0:240, :],
+            12 + 2 * t + k,
+            lambda p: sf.at[k, two, pl.ds(2 * p, 2)],
+            lambda p: rf.at[k, two, :, rows_of(p, 16), :],
+            rf.at[k, two, :, 0:240, :],
         )
 
     def pack(k):
@@ -312,7 +311,8 @@
             sf[k, lax.div(i, 4), pl.ds(8 * lax.rem(i, 4), 8)] = val.astype(BF16)
 
         loop(0, 16, body)
-        xy_start(*ab(k))
+        xy_start(*ab(0, k))
+        xy_start(*ab(1, k))
 
     arrived(0)
     arrived(1)
@@ -336,48 +336,48 @@
         all_rows(q2, k, 2, q1).wait_send()
     for i in range(4):
         far(i).wait_send()
-    for k in range(2):
-        xy_wait(*ab(k))
-
-    def xx(k):
+    def xx(t, k):
         return (
-            2 + k,
-            lambda p: xs.at[k, :, :, rows_of(p, 16), :],
-            lambda p: xr.at[k, :, pl.ds(2 * p, 2)],
-            xr.at[k, :, 0:30],
+            2 * t + k,
+            lambda p: xs.at[k, t, :, rows_of(p, 16), :],
+            lambda p: xr.at[k, t, pl.ds(2 * p, 2)],
+            xr.at[k, t, 0:30],
         )
 
     def both(ref, *at):
         return jnp.concatenate([ref[(0, *at)], ref[(1, *at)]], axis=1)
 
-    for k in range(2):
-        for c in range(2):
-            a, b, ta, tb = [both(rf, n, c) for n in range(4)]
-            b, tb = b[lanes_of(k)], tb[lanes_of(k)]
-            x = dot(a, b, NT)
-            tx = dot(jnp.concatenate([ta, a], axis=1), jnp.concatenate([b, tb], axis=1), NT)
-            xs[k, 0, c] = x.astype(BF16)
-            xs[k, 1, c] = tx.astype(BF16)
-        xy_start(*xx(k))
-
-    def zz(k):
+    for t in range(2):
+        for k in range(2):
+            xy_wait(*ab(t, k))
+        for k in range(2):
+            for c in range(2):
+                a, b = both(rf, 0, c), both(rf, 1, c)[lanes_of(k)]
+                if t == 1:
+                    ta, tb = both(rf, 2, c), both(rf, 3, c)[lanes_of(k)]
+                    a = jnp.concatenate([ta, a], axis=1)
+                    b = jnp.concatenate([b, tb], axis=1)
+                xs[k, t, c] = dot(a, b, NT).astype(BF16)
+            xy_start(*xx(t, k))
+
+    def zz(t, k):
         return (
-            k,
-            lambda p: zs.at[k, :, pl.ds(4 * slot(p), 4)],
-            lambda p: zr.at[k, :, :, rows_of(p, 32), :],
-            zr.at[k, :, :, 0:96, :],
-        )
-
-    for k in range(2):
-        xy_wait(*xx(k))
-        spread(k, xr)
-
-        def turn(r):
-            zs[k, 0, r] = get(k, r).astype(BF16)
-            zs[k, 1, r] = get(k, 512 + r).astype(BF16)
-
-        loop(0, 16, turn)
-        q_start(*zz(k))
+            5 + 2 * t + k,
+            lambda p: zs.at[k, t, pl.ds(4 * slot(p), 4)],
+            lambda p: zr.at[k, t, :, rows_of(p, 32), :],
+            zr.at[k, t, :, 0:96, :],
+        )
+
+    for t in range(2):
+        for k in range(2):
+            xy_wait(*xx(t, k))
+            spread(k, t, xr)
+
+            def turn(r):
+                zs[k, t, r] = get(k, 512 * t + r).astype(BF16)
+
+            loop(0, 16, turn)
+            q_start(*zz(t, k))
 
     hs[...] = jnp.zeros_like(hs)
 
@@ -426,7 +426,8 @@
 
     five = (4, lambda p: hs.at[rows_of(p, 64), :], lambda p: hr.at[p], hr.at[0:3])
     for k in range(2):
-        q_wait(*zz(k))
+        q_wait(*zz(0, k))
+        q_wait(*zz(1, k))
         loop(0, 2, lambda i: heads(k, i))
         q_start(*xb(k))
 
@@ -491,7 +492,8 @@
     hsum[...] = hr[0] + hr[1] + hr[2] + hr[3]
     for k in range(2):
         xy_wait(*aa(k))
-        spread(k, ar)
+        spread(k, 0, ar)
+        spread(k, 1, ar)
 
         def grad(r):
             ra = get(k, r)
@@ -522,33 +524,26 @@
     total = vb[0]
     for p in range(1, 8):
         total = total + vb[p]
-    core, row = lax.rem(q, 2), lax.div(q, 2)
-    wb[core, row, xy] = total
-
-    def swap():
-        here = wb.at[core, row, xy]
-        return rcopy(here, here, ag_s.at[0, 2], ag_r.at[0, 2], q_dev(q2))
-
-    swap().start()
-    swap().wait()
-
-    here = wb.at[core, :, xy]
+    wb[xy, q] = total.astype(BF16)
+
+    for p in (q2, q3, q1):
+        here = wb.at[xy, q]
+        rcopy(here, here, q_s.at[0], q_r.at[0], q_dev(p)).start()
+    most = wb.at[0, 0:3]
+    rcopy(most, most, q_s.at[0], q_r.at[0], q_dev(q1)).wait()
+    here = wb.at[xy]
     for p in peers:
         rcopy(here, here, xs_s.at[9], xs_r.at[9], xy_dev(p)).start()
-    most = wb.at[core, :, 0:15]
-    rcopy(most, most, xs_s.at[9], xs_r.at[9], xy_dev(lax.rem(xy + 1, 16))).wait()
-
-    share = rcopy(wb.at[core], wb.at[core], ag_s.at[0, 3], ag_r.at[0, 3], q_dev(q1))
-    share.start()
-    share.wait()
+    most = wb.at[0:15]
+    rcopy(most, most, xs_s.at[9], xs_r.at[9], xy_dev(peers[0])).wait()
 
     for p in range(4):
         for k in range(16):
             lo = 128 * (k // 4) + 32 * p + 8 * (k % 4)
-            ft[lo : lo + 4, :] = wb[p % 2, p // 2, k, 0]
-            ft[lo + 4 : lo + 8, :] = wb[p % 2, p // 2, k, 1]
+            ft[lo : lo + 4, :] = wb[k, p, 0].astype(F32)
+            ft[lo + 4 : lo + 8, :] = wb[k, p, 1].astype(F32)
             lo = 512 + 64 * p + 4 * k
-            ft[lo : lo + 4, :] = wb[p % 2, p // 2, k, 2]
+            ft[lo : lo + 4, :] = wb[k, p, 2].astype(F32)
     for t in range(6):
         cols = slice(128 * t, 128 * t + 128)
         curv_ref[:, cols] = ft[cols, :].T
@@ -604,11 +599,11 @@
             pltpu.VMEM((16, 3, 4, 128), F32),
             pltpu.VMEM((16, 3, 4, 128), F32),
             pltpu.VMEM((8, 3, 4, 128), F32),
-            pltpu.VMEM((2, 2, 16, 3, 4, 128), F32),
+            pltpu.VMEM((16, 4, 3, 4, 128), BF16),
             pltpu.VMEM((768, 128), F32),
             dma((4,)), dma((5,)), dma((5,)), dma((3, 4)), dma((3, 4)),
-            dma((10,)), dma((10,)), dma((5,)), dma((5,)),
-            dma, dma, dma, dma, dma((2,)), dma((2,)),
+            dma((16,)), dma((16,)), dma((9,)), dma((9,)),
+            dma, dma, dma, dma, dma((4,)), dma((9,)),
         ],
         compiler_params=pltpu.CompilerParams(
             collective_id=0, has_side_effects=True, vmem_limit_bytes=58 * 2**20

time: 105 us -> 101 us (0.962)
  Pallas kernels: 103 us -> 98.8 us
    pallas_call x1, Pallas kernels: 103 us -> 98.8 us  [shards(): pl.pallas_call(kernel, out_shape=(pltpu.VMEM((4, 256, 128), BF16), pltpu....]
where the time goes in v7:
time: 101 us
  Pallas kernels  98.8 us (98%)
  local copies, waits for them, and re-layouts  1.45 us (1%)
    pallas_call x1, Pallas kernels, shards(): pl.pallas_call(kernel, out_shape=(pltpu.VMEM((4, 256, 128), BF16), pltpu....  98.8 us

profile of v7, /device:TPU:1, one launch (start us, length us, event | category | flops | bytes accessed | tf_op | source)
XLA Modules:
  0.0 100.9 jit_solution(16280738624745307933)
XLA Ops:
  0.6 98.8 %shard_map.59 = (bf16[4,256,128]{2,1,0:T(8,128)(2,1)S(1)}, f32[128,768]{1,0:T(8,128)S(1)}) custom-call(bf16[4,256,128]{2,1,0:T(8,128)(2,1)} %bitcast.3, s32[1,256]{1,0:T(1,128)} %cmask_ref.1, bf16[128,768]{1,0:T(8,128)(2,1)} %w_any.1, s32[128,768]{1,0:T(8,128)} %s_any.1), custom_call_target="tpu_custom_call" | custom-call | tf_op jit(solution)/shard_map/pallas_call | solution.py:561
  99.4 0.7 copy.8
  100.1 0.7 copy.9

commit v8 on v7

--- a/solution.py
+++ b/solution.py
@@ -105,20 +105,28 @@
             device_id=to, device_id_type=MESH,
         )
 
+    peers = [
+        4 * lax.rem(lax.div(xy, 4) + dx, 4) + lax.rem(lax.rem(xy, 4) + dy, 4)
+        for dx, dy in SHIFTS
+    ]
+
     barrier = pltpu.get_barrier_semaphore()
 
     def greet(to):
         pl.semaphore_signal(barrier, inc=1, device_id=to, device_id_type=MESH)
-
-    loop(1, 16, lambda d: greet(xy_dev(lax.rem(xy + d, 16))))
-    loop(1, 8, lambda d: greet(v_dev(lax.rem(v + d, 8))))
-    loop(1, 4, lambda d: greet(q_dev(lax.rem(q + d, 4))))
 
     @pl.when(moved)
     def _():
         greet(dev(dst_c, dst_a))
         greet(dev(src_c, src_a))
 
+    for d in (4, 3, 5, 2, 6, 1, 7):
+        greet(v_dev(lax.rem(v + d, 8)))
+    for p in peers:
+        greet(xy_dev(p))
+    for d in (2, 3, 1):
+        greet(q_dev(lax.rem(q + d, 4)))
+
     loads = [
         pltpu.make_async_copy(a, b, in_s.at[k])
         for k, (a, b) in enumerate(
@@ -127,6 +135,70 @@
     ]
     for load in loads:
         load.start()
+    loads[2].wait()
+    loads[3].wait()
+
+    @pl.when(moved)
+    def _():
+        pl.semaphore_wait(barrier, 27)
+
+    @pl.when(stays)
+    def _():
+        pl.semaphore_wait(barrier, 25)
+
+    def put(k, lo, val):
+        tmp[pl.ds(2048 * k + lo, 32, stride=16), :] = val
+
+    def get(k, lo):
+        return tmp[pl.ds(2048 * k + lo, 32, stride=16), :]
+
+    def flat(k, i):
+        return pl.ds(pl.multiple_of(2048 * k + 128 * i, 128), 128)
+
+    def spread(k, t, src):
+        for i in range(4):
+            val = src[k, t, 8 * i : 8 * i + 8].astype(F32)
+            tmp[flat(k, 4 * t + i), :] = val.reshape(128, 128)
+
+    own = slot(q)
+
+    def lanes_of(k):
+        return slice(128 * k, 128 * k + 128)
+
+    def piece(p, i):
+        return pl.ds(4 * p + 2 * (i % 2), 2), lanes_of(i // 2)
+
+    def mv_pair(i):
+        return rcopy(
+            pv.at[piece(0, i)], pg.at[piece(hi, i)], mv_s.at[i], mv_r.at[i], dev(dst_c, dst_a)
+        )
+
+    def mv_mask():
+        return rcopy(cm, mk, mv_s.at[4], mv_r.at[4], dev(dst_c, dst_a))
+
+    def own_pair(i):
+        return pltpu.make_async_copy(pv.at[piece(0, i)], pg.at[piece(own, i)], mv_r.at[i])
+
+    def own_mask():
+        return pltpu.make_async_copy(cm, mk, mv_r.at[4])
+
+    def launch(i):
+        @pl.when(moved)
+        def _():
+            if i == 0:
+                mv_mask().start()
+            mv_pair(i).start()
+
+        @pl.when(stays)
+        def _():
+            if i == 0:
+                own_mask().start()
+            own_pair(i).start()
+
+    launch(0)
+    launch(1)
+    launch(2)
+
     loads[0].wait()
     loads[1].wait()
     for t in range(6):
@@ -138,68 +210,6 @@
         rows = pl.ds(pl.multiple_of(128 * t + 32 * q, 32), 32)
         wq[32 * t : 32 * t + 32, :] = wt[rows, :]
         wq[128 + 32 * t : 160 + 32 * t, :] = vt[rows, :]
-    loads[2].wait()
-    loads[3].wait()
-
-    @pl.when(moved)
-    def _():
-        pl.semaphore_wait(barrier, 27)
-
-    @pl.when(stays)
-    def _():
-        pl.semaphore_wait(barrier, 25)
-
-    def put(k, lo, val):
-        tmp[pl.ds(2048 * k + lo, 32, stride=16), :] = val
-
-    def get(k, lo):
-        return tmp[pl.ds(2048 * k + lo, 32, stride=16), :]
-
-    def flat(k, i):
-        return pl.ds(pl.multiple_of(2048 * k + 128 * i, 128), 128)
-
-    def spread(k, t, src):
-        for i in range(4):
-            val = src[k, t, 8 * i : 8 * i + 8].astype(F32)
-            tmp[flat(k, 4 * t + i), :] = val.reshape(128, 128)
-
-    own = slot(q)
-
-    def lanes_of(k):
-        return slice(128 * k, 128 * k + 128)
-
-    def piece(p, i):
-        return pl.ds(4 * p + 2 * (i % 2), 2), lanes_of(i // 2)
-
-    def mv_pair(i):
-        return rcopy(
-            pv.at[piece(0, i)], pg.at[piece(hi, i)], mv_s.at[i], mv_r.at[i], dev(dst_c, dst_a)
-        )
-
-    def mv_mask():
-        return rcopy(cm, mk, mv_s.at[4], mv_r.at[4], dev(dst_c, dst_a))
-
-    def own_pair(i):
-        return pltpu.make_async_copy(pv.at[piece(0, i)], pg.at[piece(own, i)], mv_r.at[i])
-
-    def own_mask():
-        return pltpu.make_async_copy(cm, mk, mv_r.at[4])
-
-    def launch(i):
-        @pl.when(moved)
-        def _():
-            if i == 0:
-                mv_mask().start()
-            mv_pair(i).start()
-
-        @pl.when(stays)
-        def _():
-            if i == 0:
-                own_mask().start()
-            own_pair(i).start()
-
-    launch(0)
-    launch(1)
 
     q1 = q + 1 - 2 * lax.rem(q, 2)
     q2 = lax.rem(q + 2, 4)
@@ -237,8 +247,8 @@
 
         far(i).start()
         near(i).start()
-        if i < 2:
-            launch(i + 2)
+        if i == 0:
+            launch(3)
 
     iota = lax.broadcasted_iota(jnp.int32, (1, 256), 1)
 
@@ -267,11 +277,6 @@
     def project4(k, p):
         for i in range(4):
             project(k, 4 * p + i)
-
-    peers = [
-        4 * lax.rem(lax.div(xy, 4) + dx, 4) + lax.rem(lax.rem(xy, 4) + dy, 4)
-        for dx, dy in SHIFTS
-    ]
 
     def xy_start(n, src, dst, most):
         pltpu.make_async_copy(src(xy), dst(xy), lx_s.at[n % 4]).start()
@@ -381,10 +386,10 @@
 
     hs[...] = jnp.zeros_like(hs)
 
-    def head(k, r):
-        znr = zn[4 * own + r, lanes_of(k), :]
-        x = zr[k, 0, r].astype(F32)
-        tx = zr[k, 1, r].astype(F32)
+    def heads(k):
+        zn4 = zn[pl.ds(4 * own, 4), lanes_of(k), :].reshape(512, 128)
+        x = jnp.concatenate([zr[k, 0, r] for r in range(4)], axis=1).astype(F32)
+        tx = jnp.concatenate([zr[k, 1, r] for r in range(4)], axis=1).astype(F32)
         c = x - mean0(x)
         rs = lax.rsqrt(mean0(c * c) + EPS)
         xnb = (c * rs).astype(BF16)
@@ -392,29 +397,31 @@
         slope = -0.5 * (rs * rs * rs)
         drs = slope * mean0(2.0 * c * tc)
         dxnb = (tc * rs + c * drs).astype(BF16)
-        g = dot(wt[512:640, :], znr, NT)
-        dg = dot(vt[512:640, :], znr, NT)
+        gates = dot(jnp.concatenate([wt[512:640, :], vt[512:640, :]], axis=0), zn4, NT)
         w_out = wt[640:768, :]
-        out = dot(w_out, xnb, NN)
-        dout = dot(w_out, dxnb, NN) + dot(vt[640:768, :], xnb, NN)
-        s = jax.nn.sigmoid(g)
+        outs2 = dot(jnp.concatenate([w_out, vt[640:768, :]], axis=0), xnb, NN)
+        out = outs2[:128]
+        dout = dot(w_out, dxnb, NN) + outs2[128:]
+        s = jax.nn.sigmoid(gates[:128])
         sp = s * (1.0 - s)
         y = s * out
-        ybar = (sp * dg * out + s * dout) * (1.0 / TOTAL)
+        ybar = (sp * gates[128:] * out + s * dout) * (1.0 / TOTAL)
         gbar = (ybar * out * sp).astype(BF16)
         obar = (ybar * s).astype(BF16)
         xnbar = dot(w_ref[:, 640:768], obar, NN).astype(BF16).astype(F32)
         rsbar = jnp.sum(xnbar * c, axis=0, keepdims=True)
         cbar = xnbar * rs + c * (rsbar * slope * (2.0 / 128))
-        xb4[k, r] = (cbar - mean0(cbar)).astype(BF16)
-        row = pg[4 * own + r, lanes_of(k), :].astype(F32)
-        outs[r, lanes_of(k), :] = (row + y.T).astype(BF16)
-        return dot(gbar, znr, NN), dot(obar, xnb, NT)
-
-    def heads(k, i):
-        first, second = head(k, 2 * i), head(k, 2 * i + 1)
-        hs[0:128, :] += first[0] + second[0]
-        hs[128:256, :] += first[1] + second[1]
+        xbar = (cbar - mean0(cbar)).astype(BF16)
+        for r in range(4):
+            xb4[k, r] = xbar[:, lanes_of(r)]
+        return y, gbar, obar, xnb, zn4
+
+    def rest(k, y, gbar, obar, xnb, zn4):
+        hs[0:128, :] += dot(gbar, zn4, NN)
+        hs[128:256, :] += dot(obar, xnb, NT)
+        for r in range(4):
+            row = pg[4 * own + r, lanes_of(k), :].astype(F32)
+            outs[r, lanes_of(k), :] = (row + y[:, lanes_of(r)].T).astype(BF16)
 
     def xb(k):
         return (
@@ -428,8 +435,9 @@
     for k in range(2):
         q_wait(*zz(0, k))
         q_wait(*zz(1, k))
-        loop(0, 2, lambda i: heads(k, i))
+        kept = heads(k)
         q_start(*xb(k))
+        rest(k, *kept)
 
     def back():
         return rcopy(outs, out_ref, o_s, o_r, dev(src_c, src_a))
@@ -461,23 +469,21 @@
     for k in range(2):
         xy_wait(*rr(k))
 
-    def aa(k):
+    def aa(t, k):
         return (
-            6 + k,
-            lambda p: as_.at[k, :, :, rows_of(p, 16), :],
-            lambda p: ar.at[k, :, pl.ds(2 * p, 2)],
-            ar.at[k, :, 0:30],
-        )
-
-    for c in range(2):
-        xbar = both(rx, c)
-        abar = dot(xbar, both(rf, 1, c), NN).astype(BF16)
-        bbar = dot(xbar, both(rf, 0, c), TN).astype(BF16)
+            6 + 10 * t + k,
+            lambda p: as_.at[k, t, :, rows_of(p, 16), :],
+            lambda p: ar.at[k, t, pl.ds(2 * p, 2)],
+            ar.at[k, t, 0:30],
+        )
+
+    for t in range(2):
+        for c in range(2):
+            bar = dot(both(rx, c), both(rf, 1 - t, c), TN if t else NN).astype(BF16)
+            for k in range(2):
+                as_[k, t, c] = bar[:, lanes_of(k)]
         for k in range(2):
-            as_[k, 0, c] = abar[:, lanes_of(k)]
-            as_[k, 1, c] = bbar[:, lanes_of(k)]
-    for k in range(2):
-        xy_start(*aa(k))
+            xy_start(*aa(t, k))
 
     @pl.when(moved)
     def _():
@@ -490,21 +496,23 @@
     gi[...] = jnp.zeros_like(gi)
     q_wait(*five)
     hsum[...] = hr[0] + hr[1] + hr[2] + hr[3]
-    for k in range(2):
-        xy_wait(*aa(k))
-        spread(k, 0, ar)
-        spread(k, 1, ar)
-
-        def grad(r):
-            ra = get(k, r)
-            rb = get(k, 512 + r)
-            d = (fac[k, r] * jnp.concatenate([ra, ra, rb, rb], axis=0)).astype(BF16)
-            return dot(d, zn[r, lanes_of(k), :], NN)
-
-        def grads(i):
-            gi[...] += (grad(4 * i) + grad(4 * i + 1)) + (grad(4 * i + 2) + grad(4 * i + 3))
-
-        loop(0, 4, grads)
+    def grad(t, k, r):
+        bar = get(k, 512 * t + r)
+        d = fac[k, r, 64 * t : 64 * t + 64, :] * jnp.concatenate([bar, bar], axis=0)
+        return dot(d.astype(BF16), zn[r, lanes_of(k), :], NN)
+
+    for t in range(2):
+        for k in range(2):
+            xy_wait(*aa(t, k))
+            spread(k, t, ar)
+
+            def grads(i):
+                parts = [grad(t, k, 8 * i + n) for n in range(8)]
+                while len(parts) > 1:
+                    parts = [x + y for x, y in zip(parts[::2], parts[1::2])]
+                gi[64 * t : 64 * t + 64, :] += parts[0]
+
+            loop(0, 2, grads)
 
     for p in range(16):
         us[p, 0] = gi[8 * p : 8 * p + 4, :]
@@ -602,7 +610,7 @@
             pltpu.VMEM((16, 4, 3, 4, 128), BF16),
             pltpu.VMEM((768, 128), F32),
             dma((4,)), dma((5,)), dma((5,)), dma((3, 4)), dma((3, 4)),
-            dma((16,)), dma((16,)), dma((9,)), dma((9,)),
+            dma((18,)), dma((18,)), dma((9,)), dma((9,)),
             dma, dma, dma, dma, dma((4,)), dma((9,)),
         ],
         compiler_params=pltpu.CompilerParams(

time: 101 us -> 101 us (level)
  no operation moved by 1% of the time
where the time goes in v8:
time: 101 us
  Pallas kernels  98.6 us (98%)
  local copies, waits for them, and re-layouts  1.45 us (1%)
    pallas_call x1, Pallas kernels, shards(): pl.pallas_call(kernel, out_shape=(pltpu.VMEM((4, 256, 128), BF16), pltpu....  98.6 us

profile of v8, /device:TPU:1, one launch (start us, length us, event | category | flops | bytes accessed | tf_op | source)
XLA Modules:
  0.0 100.7 jit_solution(18368970602194448366)
XLA Ops:
  0.6 98.6 %shard_map.59 = (bf16[4,256,128]{2,1,0:T(8,128)(2,1)S(1)}, f32[128,768]{1,0:T(8,128)S(1)}) custom-call(bf16[4,256,128]{2,1,0:T(8,128)(2,1)} %bitcast.3, s32[1,256]{1,0:T(1,128)} %cmask_ref.1, bf16[128,768]{1,0:T(8,128)(2,1)} %w_any.1, s32[128,768]{1,0:T(8,128)} %s_any.1), custom_call_target="tpu_custom_call" | custom-call | tf_op jit(solution)/shard_map/pallas_call | solution.py:569
  99.2 0.7 copy.8
  99.9 0.7 copy.9

commit v9 on v8

--- a/solution.py
+++ b/solution.py
@@ -174,13 +174,13 @@
         )
 
     def mv_mask():
-        return rcopy(cm, mk, mv_s.at[4], mv_r.at[4], dev(dst_c, dst_a))
+        return rcopy(cm, mk.at[0], mv_s.at[4], mv_r.at[4], dev(dst_c, dst_a))
 
     def own_pair(i):
         return pltpu.make_async_copy(pv.at[piece(0, i)], pg.at[piece(own, i)], mv_r.at[i])
 
     def own_mask():
-        return pltpu.make_async_copy(cm, mk, mv_r.at[4])
+        return pltpu.make_async_copy(cm, mk.at[0], mv_r.at[4])
 
     def launch(i):
         @pl.when(moved)
@@ -259,7 +259,7 @@
         znr = (centered * lax.rsqrt(var + EPS)).astype(BF16)
         zn[r, lanes_of(k), :] = znr
         proj = dot(wq[...], znr, NT)
-        m = mk[...].astype(F32)
+        m = mk[0].astype(F32)
         mi = jnp.sum(jnp.where(iota == 16 * xy + r, m, 0.0), axis=1, keepdims=True)
         mrow = m[:, lanes_of(k)] * mi
         for side in range(2):
@@ -583,10 +583,10 @@
             pltpu.VMEM((768, 128), BF16),
             pltpu.VMEM((256, 128), BF16),
             pltpu.VMEM((16, 256, 128), BF16),
-            pltpu.VMEM((1, 256), jnp.int32),
+            pltpu.VMEM((8, 1, 256), jnp.int32),
             pltpu.VMEM((16, 256, 128), BF16),
             pltpu.VMEM((2, 16, 128, 128), F32),
-            pltpu.VMEM((4096, 128), F32),
+            pltpu.VMEM((4224, 128), F32),
             pltpu.VMEM((2, 4, 32, 16, 128), BF16),
             pltpu.VMEM((2, 4, 2, 256, 128), BF16),
             pltpu.VMEM((2, 2, 2, 256, 128), BF16),
@@ -604,10 +604,10 @@
             pltpu.VMEM((256, 128), F32),
             pltpu.VMEM((4, 64, 128), F32),
             pltpu.VMEM((128, 128), F32),
-            pltpu.VMEM((16, 3, 4, 128), F32),
-            pltpu.VMEM((16, 3, 4, 128), F32),
-            pltpu.VMEM((8, 3, 4, 128), F32),
-            pltpu.VMEM((16, 4, 3, 4, 128), BF16),
+            pltpu.VMEM((17, 3, 4, 128), F32),
+            pltpu.VMEM((17, 3, 4, 128), F32),
+            pltpu.VMEM((9, 3, 4, 128), F32),
+            pltpu.VMEM((17, 4, 3, 4, 128), BF16),
             pltpu.VMEM((768, 128), F32),
             dma((4,)), dma((5,)), dma((5,)), dma((3, 4)), dma((3, 4)),
             dma((18,)), dma((18,)), dma((9,)), dma((9,)),

time: 101 us -> 101 us (level)
  no operation moved by 1% of the time
where the time goes in v9:
time: 101 us
  Pallas kernels  98.6 us (98%)
  local copies, waits for them, and re-layouts  1.45 us (1%)
    pallas_call x1, Pallas kernels, shards(): pl.pallas_call(kernel, out_shape=(pltpu.VMEM((4, 256, 128), BF16), pltpu....  98.6 us

profile of v9, /device:TPU:1, one launch (start us, length us, event | category | flops | bytes accessed | tf_op | source)
XLA Modules:
  0.0 100.7 jit_solution(12715191255955013162)
XLA Ops:
  0.6 98.6 %shard_map.59 = (bf16[4,256,128]{2,1,0:T(8,128)(2,1)S(1)}, f32[128,768]{1,0:T(8,128)S(1)}) custom-call(bf16[4,256,128]{2,1,0:T(8,128)(2,1)} %bitcast.3, s32[1,256]{1,0:T(1,128)} %cmask_ref.1, bf16[128,768]{1,0:T(8,128)(2,1)} %w_any.1, s32[128,768]{1,0:T(8,128)} %s_any.1), custom_call_target="tpu_custom_call" | custom-call | tf_op jit(solution)/shard_map/pallas_call | solution.py:569
  99.2 0.7 copy.8
  99.9 0.7 copy.9
